TPU v7x, 512 devices: a whole 4x8x8 slice. The times are simulated.
512 devices in a mesh: dp: 16 (over z, core), row: 8 (over y), col: 4 (over x).
Axes of the slice: x: 4, y: 8, z: 8, core: 2. Of those that a mesh axis runs over, the one named last changes fastest.
Arguments:
- token_ids: int32 [128, 4], replicated, may hold values from 0 to 81919
- slot_heads: int32 [32], replicated, may hold values from 0 to 31, each once
- embed_table: bfloat16 [81920, 2304], P('dp', ('row', 'col')), may hold values from -6 to 6
- query_weight: bfloat16 [2304, 128, 32], P('col', 'row'), may hold values from -0.125 to 0.125
- key_weight: bfloat16 [2304, 128, 32], P('col', 'row'), may hold values from -0.125 to 0.125
- value_weight: bfloat16 [2304, 128, 32], P('row', 'col'), may hold values from -0.125 to 0.125
- decay_down: bfloat16 [2304, 128], P('col'), may hold values from -0.125 to 0.125
- decay_up: bfloat16 [128, 128, 32], P(None, 'row'), may hold values from -0.5 to 0.5
- decay_bias: float32 [128, 32], P('row'), may hold values from -4 to 4
- decay_rate: float32 [128, 32], P('row'), may hold values from 0.01 to 1.5
- beta_weight: bfloat16 [2304, 32], P('col'), may hold values from -0.125 to 0.125
- init_state: float32 [128, 128, 128, 32], P('dp', 'row', 'col'), may hold values from -80 to 80
Outputs:
- readout: bfloat16 [128, 4, 128, 32], P('dp', None, 'col')
- final_state: float32 [128, 128, 128, 32], P('dp', 'row', 'col')
Inputs may be any that keep to these rules, and one draw needn't show every extreme that they name: `slot_heads`: each head once.
All inputs are finite; a program needn't handle non-finite values.
Results may differ from a plain program's by a relative error of at most 0.0022.
Values may be sent and summed in bfloat16 or wider, within the bound.
No kernel may reach another device: no remote copies, remote signals or barrier semaphores. Data moves between devices by JAX's collectives and lax.ppermute only.
A program may use at most 64 MiB of HBM per device.

v0:
```python
import math

import jax
import jax.numpy as jnp
from jax import lax
from jax.sharding import PartitionSpec as P

DK = 128
DV = 128


epsilon = 1e-06


def split_up(array, dim, length):
    shape = array.shape
    parts = array.reshape(*shape[:dim], length, shape[dim] // length, *shape[dim + 1 :])
    return jnp.moveaxis(parts, dim, 0)


def summed_on_arrival(array, axis, dim):
    parts = split_up(array, dim, lax.axis_size(axis))
    arrived = lax.all_to_all(parts, axis, split_axis=0, concat_axis=0, tiled=True)
    return arrived.astype(jnp.float32).sum(axis=0)


def from_everyone(array, axis):
    copies = jnp.broadcast_to(array, (lax.axis_size(axis), *array.shape))
    return lax.all_to_all(copies, axis, split_axis=0, concat_axis=0, tiled=True)


def joined_along(parts, dim):
    shape = list(parts.shape[1:])
    shape[dim] *= parts.shape[0]
    return jnp.moveaxis(parts, 0, dim).reshape(shape)


def gathered_copies(array, axis, dim):
    parts = from_everyone(array, axis)
    return joined_along(parts, dim)


def taken_together(array, axis):
    return from_everyone(array, axis).sum(axis=0)


def packed_total(arrays, axis):
    ends = [0]
    for a in arrays:
        ends.append(ends[-1] + a.size)
    so_far = taken_together(jnp.concatenate([a.ravel() for a in arrays]), axis)
    return tuple((so_far[b:e].reshape(a.shape) for a, b, e in zip(arrays, ends, ends[1:])))


def sent_together(arrays, axis, split_dim, concat_dim, along):
    widths = [a.shape[along] for a in arrays]
    both = jnp.concatenate(arrays, axis=along)
    filled = lax.all_to_all(both, axis, split_axis=split_dim, concat_axis=concat_dim, tiled=True)
    return tuple(jnp.split(filled, [sum(widths[:k]) for k in range(1, len(widths))], axis=along))


def local_steps(query, keys, values, alpha, beta, current, step_count):
    clip_norm = math.sqrt(DK * DV)
    highest = lax.Precision.HIGHEST
    outputs = []
    for step in range(step_count):
        key_now = keys[:, step]
        query_now = query[:, step]
        gate_now = beta[:, step]
        khat = key_now / jnp.sqrt(jnp.sum(key_now * key_now, axis=1) + epsilon)[:, None, :]
        decayed = alpha[:, step][:, :, None, :] * current
        weights_read = jnp.einsum("bih,bijh->bjh", khat, decayed, precision=highest)
        probe = jnp.einsum("bih,bijh->bjh", query_now, decayed, precision=highest)
        cross = jnp.sum(khat * query_now, axis=1)
        residue = values[:, step] - weights_read
        updated = (
            decayed + gate_now[:, None, None, :] * khat[:, :, None, :] * residue[:, None, :, :]
        )
        early = probe + (gate_now * cross)[:, None, :] * residue
        norm_total = jnp.sqrt(jnp.sum(updated * updated, axis=(1, 2)))
        factor = 1.0 / jnp.maximum(1.0, norm_total / clip_norm)
        current = updated * factor[:, None, None, :]
        outputs.append(early * factor[:, None, :])
    return (jnp.stack(outputs, axis=1), current)


def shards(
    token_ids,
    slot_heads,
    embed_table,
    query_weight,
    key_weight,
    value_weight,
    decay_down,
    decay_up,
    decay_bias,
    decay_rate,
    beta_weight,
    init_state,
):
    batch_rows = init_state.shape[0]
    step_count = token_ids.shape[1]
    vocab_rows = embed_table.shape[0]
    vocab_start = lax.axis_index("dp") * vocab_rows
    local_ids = token_ids - vocab_start
    inside = (local_ids >= 0) & (local_ids < vocab_rows)
    picked = jnp.take(embed_table, jnp.clip(local_ids, 0, vocab_rows - 1), axis=0)
    shard = summed_on_arrival(
        jnp.where(inside[:, :, None], picked.astype(jnp.float32), 0.0).astype(jnp.bfloat16), "dp", 0
    ).astype(jnp.bfloat16)
    embedded = gathered_copies(shard, ("row", "col"), 2)
    token_count = batch_rows * step_count
    flat_tokens = embedded.reshape(token_count, -1)
    col_width = query_weight.shape[0]
    key_part = query_weight.shape[1]
    heads = query_weight.shape[2]
    columns = lax.dynamic_slice_in_dim(flat_tokens, lax.axis_index("col") * col_width, col_width, 1)
    query_sum = jnp.dot(
        columns, query_weight.reshape(col_width, -1), preferred_element_type=jnp.float32
    )
    key_sum = jnp.dot(
        columns, key_weight.reshape(col_width, -1), preferred_element_type=jnp.float32
    )
    low_sum = jnp.dot(columns, decay_down, preferred_element_type=jnp.float32)
    beta_sum = jnp.dot(columns, beta_weight, preferred_element_type=jnp.float32)
    query, keys, low_rank, logits = packed_total((query_sum, key_sum, low_sum, beta_sum), "col")
    low_rank = low_rank.astype(jnp.bfloat16)
    inner_width = decay_up.shape[0]
    gate_input = jnp.dot(
        low_rank, decay_up.reshape(inner_width, -1), preferred_element_type=jnp.float32
    )
    gate_input = gate_input.reshape(batch_rows, step_count, key_part, heads)
    alpha = jnp.exp(-decay_rate * jax.nn.softplus(gate_input + decay_bias))
    query = query.reshape(batch_rows, step_count, key_part, heads) * DK ** (-0.5)
    keys = keys.reshape(batch_rows, step_count, key_part, heads)
    beta = jax.nn.sigmoid(logits).reshape(batch_rows, step_count, heads)
    row_width = value_weight.shape[0]
    value_part = value_weight.shape[1]
    row_columns = lax.dynamic_slice_in_dim(
        flat_tokens, lax.axis_index("row") * row_width, row_width, 1
    )
    values = jnp.dot(
        row_columns, value_weight.reshape(row_width, -1), preferred_element_type=jnp.float32
    )
    values = values.reshape(batch_rows, step_count, value_part, heads)
    query = jnp.take(query, slot_heads, axis=3)
    keys = jnp.take(keys, slot_heads, axis=3)
    values = jnp.take(values, slot_heads, axis=3)
    alpha = jnp.take(alpha, slot_heads, axis=3)
    beta = jnp.take(beta, slot_heads, axis=2)
    row_index = lax.axis_index("row")
    col_index = lax.axis_index("col")
    row_share = heads // lax.axis_size("row")
    share = row_share // lax.axis_size("col")
    query_rows, keys_rows, alpha_rows = sent_together((query, keys, alpha), "row", 3, 2, 0)
    query_own = lax.dynamic_slice_in_dim(query_rows, col_index * share, share, 3)
    keys_own = lax.dynamic_slice_in_dim(keys_rows, col_index * share, share, 3)
    alpha_own = lax.dynamic_slice_in_dim(alpha_rows, col_index * share, share, 3)
    values_block = summed_on_arrival(values.astype(jnp.bfloat16), "row", 3)
    values_own = lax.all_to_all(values_block, "col", split_axis=3, concat_axis=2, tiled=True)
    beta_own = lax.dynamic_slice_in_dim(beta, row_index * row_share + col_index * share, share, 2)
    state_own = lax.all_to_all(
        lax.all_to_all(init_state, "row", split_axis=3, concat_axis=1, tiled=True),
        "col",
        split_axis=3,
        concat_axis=2,
        tiled=True,
    )
    stacked, finished = local_steps(
        query_own, keys_own, values_own, alpha_own, beta_own, state_own, step_count
    )
    returned = lax.all_to_all(
        stacked.astype(jnp.bfloat16), "col", split_axis=2, concat_axis=3, tiled=True
    )
    all_slots = gathered_copies(returned, "row", 3)
    head_order = jnp.zeros_like(all_slots).at[..., slot_heads].set(all_slots)
    state_back = lax.all_to_all(finished, "col", split_axis=2, concat_axis=3, tiled=True)
    state_back = lax.all_to_all(state_back, "row", split_axis=1, concat_axis=3, tiled=True)
    return (head_order, state_back)


def solution(mesh):
    in_specs = (
        P(),
        P(),
        P("dp", ("row", "col")),
        P("col", "row", None),
        P("col", "row", None),
        P("row", "col", None),
        P("col", None),
        P(None, "row", None),
        P("row", None),
        P("row", None),
        P("col", None),
        P("dp", "row", "col", None),
    )
    out_specs = (P("dp", None, "col", None), P("dp", "row", "col", None))
    return jax.shard_map(shards, mesh=mesh, in_specs=in_specs, out_specs=out_specs, check_vma=False)
```

profile of v0, /device:TPU:2, one launch (start us, length us, event | category | flops | bytes accessed | tf_op | source)
XLA Modules:
  0.0 209.5 jit_solution(7918565709936180214)
XLA Ops:
  6.2 1.7 select_convert_fusion.1
  7.9 10.4 %all-to-all-start = ((bf16[16,8,4,72]{3,2,1,0:T(4,128)(2,1)}), bf16[16,8,4,72]{3,2,1,0:T(4,128)(2,1)S(1)}, u32[]{:S(2)}, u32[]{:S(2)}) async-start(bf16[16,8,4,72]{3,2,1,0:T(4,128)(2,1)} %select_convert_fusion.1), calls=%async_computation | async-start | bytes 262144 | tf_op jit(solution)/shard_map/all_to_all | solution.py:23
  18.4 8.5 %all-to-all-done = bf16[16,8,4,72]{3,2,1,0:T(4,128)(2,1)S(1)} async-done(((bf16[16,8,4,72]{3,2,1,0:T(4,128)(2,1)}), bf16[16,8,4,72]{3,2,1,0:T(4,128)(2,1)S(1)}, u32[]{:S(2)}, u32[]{:S(2)}) %all-to-all-start) | async-done | bytes 73760 | tf_op jit(solution)/shard_map/all_to_all | solution.py:23
  27.8 10.2 %all-to-all-start.1 = ((bf16[32,8,4,72]{3,2,1,0:T(4,128)(2,1)}), bf16[32,8,4,72]{3,2,1,0:T(4,128)(2,1)S(1)}, u32[]{:S(2)}, u32[]{:S(2)}) async-start(bf16[32,8,4,72]{3,2,1,0:T(4,128)(2,1)} %broadcast_in_dim.110), calls=%async_computation.1 | async-start | bytes 524288 | tf_op jit(solution)/shard_map/all_to_all | solution.py:29
  38.1 12.0 %all-to-all-done.1 = bf16[32,8,4,72]{3,2,1,0:T(4,128)(2,1)S(1)} async-done(((bf16[32,8,4,72]{3,2,1,0:T(4,128)(2,1)}), bf16[32,8,4,72]{3,2,1,0:T(4,128)(2,1)S(1)}, u32[]{:S(2)}, u32[]{:S(2)}) %all-to-all-start.1) | async-done | bytes 147488 | tf_op jit(solution)/shard_map/all_to_all | solution.py:29
  54.4 3.4 %all-to-all-start.6 = ((bf16[8,2,2048]{2,1,0:T(2,128)(2,1)}), bf16[8,2,2048]{2,1,0:T(2,128)(2,1)S(1)}, u32[]{:S(2)}, u32[]{:S(2)}) async-start(bf16[8,2,2048]{2,1,0:T(2,128)(2,1)} %reshape.1140), calls=%async_computation.6 | async-start | bytes 131072 | tf_op jit(solution)/shard_map/all_to_all | solution.py:23
  58.0 8.1 %all-to-all-done.6 = bf16[8,2,2048]{2,1,0:T(2,128)(2,1)S(1)} async-done(((bf16[8,2,2048]{2,1,0:T(2,128)(2,1)}), bf16[8,2,2048]{2,1,0:T(2,128)(2,1)S(1)}, u32[]{:S(2)}, u32[]{:S(2)}) %all-to-all-start.6) | async-done | bytes 65568 | tf_op jit(solution)/shard_map/all_to_all | solution.py:23
  67.0 5.3 %all-to-all-start.7 = ((f32[4,1,1024]{2,1,0:T(1,128)}), f32[4,1,1024]{2,1,0:T(1,128)S(1)}, u32[]{:S(2)}, u32[]{:S(2)}) async-start(f32[4,1,1024]{2,1,0:T(1,128)} %reshape.1142), calls=%async_computation.7 | async-start | bytes 32768 | tf_op jit(solution)/shard_map/all_to_all | solution.py:160
  72.3 3.9 %all-to-all-done.7 = f32[4,1,1024]{2,1,0:T(1,128)S(1)} async-done(((f32[4,1,1024]{2,1,0:T(1,128)}), f32[4,1,1024]{2,1,0:T(1,128)S(1)}, u32[]{:S(2)}, u32[]{:S(2)}) %all-to-all-start.7) | async-done | bytes 16416 | tf_op jit(solution)/shard_map/all_to_all | solution.py:160
  77.3 4.9 %all-to-all-start.2 = ((f32[4,1,37888]{2,1,0:T(1,128)}), f32[4,1,37888]{2,1,0:T(1,128)S(1)}, u32[]{:S(2)}, u32[]{:S(2)}) async-start(f32[4,1,37888]{2,1,0:T(1,128)} %broadcast_in_dim.111), calls=%async_computation.2 | async-start | bytes 1212416 | tf_op jit(solution)/shard_map/all_to_all | solution.py:29
  82.8 3.1 %copy.235 = f32[8,16,32,32]{2,1,0,3:T(8,128)S(1)} copy(f32[8,16,32,32]{3,2,1,0:T(8,128)} %param.25) | data formatting | bytes 1048576 | tf_op args[11]
  89.3 4.1 %all-to-all-start.4 = ((f32[8,1,16384]{2,1,0:T(1,128)}), f32[8,1,16384]{2,1,0:T(1,128)}, u32[]{:S(2)}, u32[]{:S(2)}) async-start(f32[8,1,16384]{2,1,0:T(1,128)} %reshape.1138), calls=%async_computation.4 | async-start | bytes 1048576 | tf_op jit(solution)/shard_map/all_to_all | solution.py:163
  99.7 7.7 %all-to-all-done.4 = f32[8,1,16384]{2,1,0:T(1,128)} async-done(((f32[8,1,16384]{2,1,0:T(1,128)}), f32[8,1,16384]{2,1,0:T(1,128)}, u32[]{:S(2)}, u32[]{:S(2)}) %all-to-all-start.4) | async-done | bytes 524320 | tf_op jit(solution)/shard_map/all_to_all | solution.py:163
  107.4 4.2 %all-to-all-start.3 = ((f32[8,1,6144]{2,1,0:T(1,128)}), f32[8,1,6144]{2,1,0:T(1,128)}, u32[]{:S(2)}, u32[]{:S(2)}) async-start(f32[8,1,6144]{2,1,0:T(1,128)} %reshape.1136), calls=%async_computation.3 | async-start | bytes 393216 | tf_op jit(solution)/shard_map/all_to_all | solution.py:58
  113.9 3.0 %reduce.19 = f32[8,16384]{1,0:T(8,128)S(1)} reduce(f32[8,1,16384]{2,1,0:T(1,128)} %all-to-all-done.4, f32[]{:T(128)} %broadcast.832), dimensions={1}, to_apply=%all_to_all.113.reduce_sub_computation | reduce | bytes 1048580 | tf_op jit(solution)/shard_map/all_to_all | solution.py:163
  119.1 3.0 %copy.238 = f32[8,128,32,4]{1,2,0,3:T(8,128)} copy(f32[8,128,32,4]{2,1,3,0:T(8,128)} %bitcast.357) | data formatting | bytes 1048576 | tf_op jit(solution)/shard_map/all_to_all | solution.py:163
  122.1 4.8 %all-to-all-start.5 = ((f32[8,128,32,4]{1,2,0,3:T(8,128)}), f32[8,128,32,4]{1,2,0,3:T(8,128)S(1)}, u32[]{:S(2)}, u32[]{:S(2)}) async-start(f32[8,128,32,4]{1,2,0,3:T(8,128)} %copy.238), calls=%async_computation.5 | async-start | bytes 1048576 | tf_op jit(solution)/shard_map/all_to_all | solution.py:162
  126.9 2.1 reduce.18
  131.5 2.4 %copy.242 = f32[8,4,8,16,4]{3,2,0,4,1:T(8,128)} copy(f32[8,4,8,16,4]{0,3,4,2,1:T(8,128)} %get-tuple-element.40) | data formatting | bytes 131072 | tf_op jit(solution)/shard_map/split | solution.py:59
  150.9 4.8 %all-to-all-start.8 = ((bf16[4,2,512]{2,1,0:T(2,128)(2,1)}), bf16[4,2,512]{2,1,0:T(2,128)(2,1)S(1)}, u32[]{:S(2)}, u32[]{:S(2)}) async-start(bf16[4,2,512]{2,1,0:T(2,128)(2,1)} %reshape.1144), calls=%async_computation.8 | async-start | bytes 16384 | tf_op jit(solution)/shard_map/all_to_all | solution.py:172
  157.7 2.0 all-to-all-done.8
  159.6 4.8 %all-to-all-start.10 = ((f32[8,128,128,1]{1,0,3,2:T(8,128)}), f32[8,128,128,1]{1,0,3,2:T(8,128)S(1)}, u32[]{:S(2)}, u32[]{:S(2)}) async-start(f32[8,128,128,1]{1,0,3,2:T(8,128)} %copy.259), calls=%async_computation.10 | async-start | bytes 1048576 | tf_op jit(solution)/shard_map/all_to_all | solution.py:177
  165.7 5.4 %all-to-all-done.10 = f32[8,128,128,1]{1,0,3,2:T(8,128)S(1)} async-done(((f32[8,128,128,1]{1,0,3,2:T(8,128)}), f32[8,128,128,1]{1,0,3,2:T(8,128)S(1)}, u32[]{:S(2)}, u32[]{:S(2)}) %all-to-all-start.10) | async-done | bytes 524320 | tf_op jit(solution)/shard_map/all_to_all | solution.py:177
  171.1 6.9 %all-to-all-start.9 = ((bf16[8,2,2048]{2,1,0:T(2,128)(2,1)}), bf16[8,2,2048]{2,1,0:T(2,128)(2,1)S(1)}, u32[]{:S(2)}, u32[]{:S(2)}) async-start(bf16[8,2,2048]{2,1,0:T(2,128)(2,1)} %reshape.1146), calls=%async_computation.9 | async-start | bytes 131072 | tf_op jit(solution)/shard_map/all_to_all | solution.py:29
  178.0 2.3 %copy.261 = f32[8,128,32,4]{2,3,0,1:T(4,128)S(1)} copy(f32[8,128,32,4]{1,0,2,3:T(8,128)S(1)} %bitcast.364) | data formatting | bytes 1048576 | tf_op jit(solution)/shard_map/all_to_all | solution.py:177
  180.3 2.2 %reshape.1148 = f32[8,1,16384]{2,1,0:T(1,128)} reshape(f32[128,8,4,32]{3,2,1,0:T(4,128)S(1)} %bitcast.355) | data formatting | bytes 1048576
  182.4 4.0 %all-to-all-done.9 = bf16[8,2,2048]{2,1,0:T(2,128)(2,1)S(1)} async-done(((bf16[8,2,2048]{2,1,0:T(2,128)(2,1)}), bf16[8,2,2048]{2,1,0:T(2,128)(2,1)S(1)}, u32[]{:S(2)}, u32[]{:S(2)}) %all-to-all-start.9) | async-done | bytes 65568 | tf_op jit(solution)/shard_map/all_to_all | solution.py:29
  186.4 3.5 %all-to-all-start.11 = ((f32[8,1,16384]{2,1,0:T(1,128)}), f32[8,1,16384]{2,1,0:T(1,128)S(1)}, u32[]{:S(2)}, u32[]{:S(2)}) async-start(f32[8,1,16384]{2,1,0:T(1,128)} %reshape.1148), calls=%async_computation.11 | async-start | bytes 1048576 | tf_op jit(solution)/shard_map/all_to_all | solution.py:178
  190.1 1.9 scatter_fusion
  193.0 10.1 %all-to-all-done.11 = f32[8,1,16384]{2,1,0:T(1,128)S(1)} async-done(((f32[8,1,16384]{2,1,0:T(1,128)}), f32[8,1,16384]{2,1,0:T(1,128)S(1)}, u32[]{:S(2)}, u32[]{:S(2)}) %all-to-all-start.11) | async-done | bytes 524320 | tf_op jit(solution)/shard_map/all_to_all | solution.py:178
  203.1 1.9 reduce.21
  207.6 1.9 copy.265
  (152 shorter events, 53.7 us)
Async XLA Ops:
  0.6 51.0 %copy-start = (bf16[288,32,32]{0,2,1:T(8,128)(2,1)S(1)}, bf16[288,32,32]{0,2,1:T(8,128)(2,1)}, u32[]{:S(2)}) copy-start(bf16[288,32,32]{0,2,1:T(8,128)(2,1)} %param.19) | copy-start | bytes 1769476
  0.6 17.7 %copy-start.9 = (s32[32]{0:T(128)S(1)}, s32[32]{0:T(128)}, u32[]{:S(2)}) copy-start(s32[32]{0:T(128)} %param.15) | copy-start | bytes 388
  4.8 46.2 %copy-start.1 = (bf16[576,16,32]{0,2,1:T(8,128)(2,1)S(1)}, bf16[576,16,32]{0,2,1:T(8,128)(2,1)}, u32[]{:S(2)}) copy-start(bf16[576,16,32]{0,2,1:T(8,128)(2,1)} %param.18) | copy-start | bytes 1769476
  4.8 46.5 %copy-start.2 = (bf16[576,16,32]{0,2,1:T(8,128)(2,1)S(1)}, bf16[576,16,32]{0,2,1:T(8,128)(2,1)}, u32[]{:S(2)}) copy-start(bf16[576,16,32]{0,2,1:T(8,128)(2,1)} %param.17) | copy-start | bytes 1769476
  6.2 44.4 %copy-start.5 = (bf16[576,32]{0,1:T(8,128)(2,1)S(1)}, bf16[576,32]{0,1:T(8,128)(2,1)}, u32[]{:S(2)}) copy-start(bf16[576,32]{0,1:T(8,128)(2,1)} %param.24) | copy-start | bytes 110596
  7.9 19.1 %all-to-all-start = ((bf16[16,8,4,72]{3,2,1,0:T(4,128)(2,1)}), bf16[16,8,4,72]{3,2,1,0:T(4,128)(2,1)S(1)}, u32[]{:S(2)}, u32[]{:S(2)}) async-start(bf16[16,8,4,72]{3,2,1,0:T(4,128)(2,1)} %select_convert_fusion.1), calls=%async_computation | async-start | bytes 262144 | tf_op jit(solution)/shard_map/all_to_all | solution.py:23
  27.8 22.3 %all-to-all-start.1 = ((bf16[32,8,4,72]{3,2,1,0:T(4,128)(2,1)}), bf16[32,8,4,72]{3,2,1,0:T(4,128)(2,1)S(1)}, u32[]{:S(2)}, u32[]{:S(2)}) async-start(bf16[32,8,4,72]{3,2,1,0:T(4,128)(2,1)} %broadcast_in_dim.110), calls=%async_computation.1 | async-start | bytes 524288 | tf_op jit(solution)/shard_map/all_to_all | solution.py:29
  51.3 6.5 %copy-start.4 = (bf16[576,128]{1,0:T(8,128)(2,1)S(1)}, bf16[576,128]{1,0:T(8,128)(2,1)}, u32[]{:S(2)}) copy-start(bf16[576,128]{1,0:T(8,128)(2,1)} %param.20) | copy-start | bytes 442372
  53.3 29.5 %copy-start.6 = (f32[16,32]{1,0:T(8,128)S(1)}, f32[16,32]{1,0:T(8,128)}, u32[]{:S(2)}) copy-start(f32[16,32]{1,0:T(8,128)} %param.23) | copy-start | bytes 6148
  54.4 11.7 %all-to-all-start.6 = ((bf16[8,2,2048]{2,1,0:T(2,128)(2,1)}), bf16[8,2,2048]{2,1,0:T(2,128)(2,1)S(1)}, u32[]{:S(2)}, u32[]{:S(2)}) async-start(bf16[8,2,2048]{2,1,0:T(2,128)(2,1)} %reshape.1140), calls=%async_computation.6 | async-start | bytes 131072 | tf_op jit(solution)/shard_map/all_to_all | solution.py:23
  67.0 9.2 %all-to-all-start.7 = ((f32[4,1,1024]{2,1,0:T(1,128)}), f32[4,1,1024]{2,1,0:T(1,128)S(1)}, u32[]{:S(2)}, u32[]{:S(2)}) async-start(f32[4,1,1024]{2,1,0:T(1,128)} %reshape.1142), calls=%async_computation.7 | async-start | bytes 32768 | tf_op jit(solution)/shard_map/all_to_all | solution.py:160
  77.3 12.0 %all-to-all-start.2 = ((f32[4,1,37888]{2,1,0:T(1,128)}), f32[4,1,37888]{2,1,0:T(1,128)S(1)}, u32[]{:S(2)}, u32[]{:S(2)}) async-start(f32[4,1,37888]{2,1,0:T(1,128)} %broadcast_in_dim.111), calls=%async_computation.2 | async-start | bytes 1212416 | tf_op jit(solution)/shard_map/all_to_all | solution.py:29
  85.9 8.2 %copy-start.8 = (f32[16,32]{1,0:T(8,128)S(1)}, f32[16,32]{1,0:T(8,128)}, u32[]{:S(2)}) copy-start(f32[16,32]{1,0:T(8,128)} %param.22) | copy-start | bytes 6148
  87.7 6.5 %copy-start.7 = (bf16[128,16,32]{0,2,1:T(8,128)(2,1)S(1)}, bf16[128,16,32]{0,2,1:T(8,128)(2,1)}, u32[]{:S(2)}) copy-start(bf16[128,16,32]{0,2,1:T(8,128)(2,1)} %param.21) | copy-start | bytes 393220
  89.3 18.1 %all-to-all-start.4 = ((f32[8,1,16384]{2,1,0:T(1,128)}), f32[8,1,16384]{2,1,0:T(1,128)}, u32[]{:S(2)}, u32[]{:S(2)}) async-start(f32[8,1,16384]{2,1,0:T(1,128)} %reshape.1138), calls=%async_computation.4 | async-start | bytes 1048576 | tf_op jit(solution)/shard_map/all_to_all | solution.py:163
  94.0 0.7 copy-start.3
  107.4 14.7 %all-to-all-start.3 = ((f32[8,1,6144]{2,1,0:T(1,128)}), f32[8,1,6144]{2,1,0:T(1,128)}, u32[]{:S(2)}, u32[]{:S(2)}) async-start(f32[8,1,6144]{2,1,0:T(1,128)} %reshape.1136), calls=%async_computation.3 | async-start | bytes 393216 | tf_op jit(solution)/shard_map/all_to_all | solution.py:58
  122.1 16.4 %all-to-all-start.5 = ((f32[8,128,32,4]{1,2,0,3:T(8,128)}), f32[8,128,32,4]{1,2,0,3:T(8,128)S(1)}, u32[]{:S(2)}, u32[]{:S(2)}) async-start(f32[8,128,32,4]{1,2,0,3:T(8,128)} %copy.238), calls=%async_computation.5 | async-start | bytes 1048576 | tf_op jit(solution)/shard_map/all_to_all | solution.py:162
  150.9 8.8 %all-to-all-start.8 = ((bf16[4,2,512]{2,1,0:T(2,128)(2,1)}), bf16[4,2,512]{2,1,0:T(2,128)(2,1)S(1)}, u32[]{:S(2)}, u32[]{:S(2)}) async-start(bf16[4,2,512]{2,1,0:T(2,128)(2,1)} %reshape.1144), calls=%async_computation.8 | async-start | bytes 16384 | tf_op jit(solution)/shard_map/all_to_all | solution.py:172
  159.6 11.4 %all-to-all-start.10 = ((f32[8,128,128,1]{1,0,3,2:T(8,128)}), f32[8,128,128,1]{1,0,3,2:T(8,128)S(1)}, u32[]{:S(2)}, u32[]{:S(2)}) async-start(f32[8,128,128,1]{1,0,3,2:T(8,128)} %copy.259), calls=%async_computation.10 | async-start | bytes 1048576 | tf_op jit(solution)/shard_map/all_to_all | solution.py:177
  171.1 15.3 %all-to-all-start.9 = ((bf16[8,2,2048]{2,1,0:T(2,128)(2,1)}), bf16[8,2,2048]{2,1,0:T(2,128)(2,1)S(1)}, u32[]{:S(2)}, u32[]{:S(2)}) async-start(bf16[8,2,2048]{2,1,0:T(2,128)(2,1)} %reshape.1146), calls=%async_computation.9 | async-start | bytes 131072 | tf_op jit(solution)/shard_map/all_to_all | solution.py:29
  186.4 16.7 %all-to-all-start.11 = ((f32[8,1,16384]{2,1,0:T(1,128)}), f32[8,1,16384]{2,1,0:T(1,128)S(1)}, u32[]{:S(2)}, u32[]{:S(2)}) async-start(f32[8,1,16384]{2,1,0:T(1,128)} %reshape.1148), calls=%async_computation.11 | async-start | bytes 1048576 | tf_op jit(solution)/shard_map/all_to_all | solution.py:178
where the time goes:
time: 211 us; the launch traced here: 210 us
  starting transfers between devices  67.3 us (32%)
  waiting for transfers between devices  61.9 us (29%)
  local copies, waits for them, and re-layouts  51.7 us (25%)
  other arithmetic  17.2 us (8%)
  matrix products  10.1 us (5%)
    all_to_all x3, starting transfers between devices, from_everyone(): return lax.all_to_all(copies, axis, split_axis=0, concat_axis=0, tiled=True)  22.1 us
    unnamed x42, local copies, waits for them, and re-layouts  20.3 us
    all_to_all x2, waiting for transfers between devices, summed_on_arrival(): lax.all_to_all(parts, axis, split_axis=0, concat_axis=0, tiled=True)  16.6 us
    all_to_all x3, waiting for transfers between devices, from_everyone(): return lax.all_to_all(copies, axis, split_axis=0, concat_axis=0, tiled=True)  16.2 us
    all_to_all x2, starting transfers between devices, summed_on_arrival(): lax.all_to_all(parts, axis, split_axis=0, concat_axis=0, tiled=True)  13.8 us
    all_to_all x1, waiting for transfers between devices, shards(): lax.all_to_all(state_back, 'row', split_axis=1, concat_axis=3, tiled=True)  10.1 us
    split x7, local copies, waits for them, and re-layouts, sent_together(): jnp.split(filled, [sum(widths[:k]) for k in range(1, len(widths))], axis=...  8.11 us
    all_to_all x1, waiting for transfers between devices, shards(): lax.all_to_all(init_state, 'row', split_axis=3, concat_axis=1, tiled=True)  7.75 us
  transfers between devices with their start and end apart: 12, of which 10 were waited for; matrix products, arithmetic and copies ran while one was open for 22% of the time, Pallas kernels for 0%

commit v1 on v0

v1 whole, which is shorter than its diff:
```python
import math

import jax
import jax.numpy as jnp
from jax import lax
from jax.experimental import pallas as pl
from jax.experimental.pallas import tpu as pltpu
from jax.sharding import PartitionSpec as P

DK = 128
DV = 128
EPSILON = 1e-06
INTERPRET = False

F32 = jnp.float32
BF16 = jnp.bfloat16
BOTH = ("row", "col")
NT = (((1,), (1,)), ((), ()))
NN = (((1,), (0,)), ((), ()))
TN = (((0,), (0,)), ((), ()))


def lanes(shape):
    return lax.broadcasted_iota(jnp.int32, shape, len(shape) - 1)


def rows_of(shape):
    return lax.broadcasted_iota(jnp.int32, shape, len(shape) - 2)


def exchange(array, axis):
    return lax.all_to_all(array, axis, split_axis=0, concat_axis=0, tiled=True)


def pick_kernel(ids_ref, table_ref, out_ref, onehot_ref):
    steps, streams = ids_ref.shape
    feats, vocab = table_ref.shape
    groups = out_ref.shape[0]
    start = lax.axis_index("dp") * vocab
    chunk = onehot_ref.shape[1]
    columns = jnp.broadcast_to((ids_ref[...] - start).astype(F32)[:, None, :], (steps, 8, streams))
    columns = [columns[t].T.astype(jnp.int32)[:, 0:1] for t in range(steps)]
    total = None
    for part in range(vocab // chunk):
        position = lanes((streams, chunk)) + part * chunk
        for t in range(steps):
            hit = columns[t] == position
            onehot_ref[t * streams : (t + 1) * streams, :] = jnp.where(hit, 1.0, 0.0).astype(BF16)
        found = lax.dot_general(
            onehot_ref[...], table_ref[:, part * chunk : (part + 1) * chunk], NT, preferred_element_type=F32
        )
        total = found if total is None else total + found
    wide = jnp.concatenate([total, jnp.zeros((total.shape[0], 128 - feats), F32)], axis=1)
    for t in range(steps):
        block = wide[t * streams : (t + 1) * streams].reshape(groups, 8, 128)
        if t % 2 == 0:
            kept = block
        else:
            pair = jnp.concatenate([kept, block], axis=1)
            out_ref[:, (t - 1) * 8 : (t + 1) * 8, :] = pair.astype(BF16)


def pack_state_kernel(state_ref, out_ref, turned_ref):
    heads = state_ref.shape[3]
    for hi in range(2):
        for i in range(16):
            block = state_ref[hi * 4 : hi * 4 + 4, i].reshape(128, heads)
            turned_ref[pl.ds(hi * 16 + i, heads, stride=32), :] = block.T
    whole = turned_ref[...].reshape(heads, 32, 128)
    upper = whole.astype(BF16)
    out_ref[:, 0:32, :] = upper
    out_ref[:, 32:64, :] = (whole - upper.astype(F32)).astype(BF16)


def add_tokens_kernel(arrived_ref, packed_ref, out_ref, own_ref, sems):
    del packed_ref
    total = arrived_ref[0].astype(F32)
    for k in range(1, arrived_ref.shape[0]):
        total = total + arrived_ref[k].astype(F32)
    own_ref[...] = total.astype(BF16)
    peers = out_ref.shape[0]
    copies = [
        pltpu.make_async_copy(own_ref, out_ref.at[p, 64:96, :], sems.at[p]) for p in range(peers)
    ]
    for copy in copies:
        copy.start()
    for copy in copies:
        copy.wait()


def side_by_side(blocks, width):
    count = (len(blocks) * width + 127) // 128
    tiles = [None] * count
    lane = lanes(blocks[0].shape)
    for k, block in enumerate(blocks):
        at, shift = divmod(k * width, 128)
        rolled = pltpu.roll(block, shift, 1) if shift else block
        low = jnp.where(lane >= shift, rolled, 0.0)
        tiles[at] = low if tiles[at] is None else tiles[at] + low
        if shift + width > 128:
            tiles[at + 1] = jnp.where(lane < shift, rolled, 0.0)
    return jnp.concatenate(tiles, axis=1)


def project_kernel(
    heads_ref, arrived_ref, query_ref, key_ref, value_ref, down_ref, up_ref, bias_ref, rate_ref, beta_ref,
    out_ref, mixed_ref,
):
    col = lax.axis_index("col")
    row = lax.axis_index("row")
    width = query_ref.shape[1] // 8

    def features(first, count):
        blocks = [arrived_ref[first + k, 64:96, :].astype(F32) for k in range(count)]
        return side_by_side(blocks, width)[:, : count * width].astype(BF16)

    own = features(col * 8, 8)
    own_four = jnp.concatenate([own] * 4, axis=0)
    across = features(row * 4, 4)
    across_four = jnp.concatenate([across] * 4, axis=0)

    low = lax.dot_general(own, down_ref[...], NN, preferred_element_type=F32)
    low_upper = low.astype(BF16)
    low_rest = (low - low_upper.astype(F32)).astype(BF16)
    query = lax.dot_general(query_ref[...], own_four, NT, preferred_element_type=F32)
    key = lax.dot_general(key_ref[...], own_four, NT, preferred_element_type=F32)
    gate = lax.dot_general(
        up_ref[...], jnp.concatenate([low_upper] * 4, axis=0), NT, preferred_element_type=F32
    ) + lax.dot_general(
        up_ref[...], jnp.concatenate([low_rest] * 4, axis=0), NT, preferred_element_type=F32
    )
    beta = lax.dot_general(beta_ref[...], own_four, NT, preferred_element_type=F32)
    lane = lanes((32, 128))
    first = jnp.where(col == 0, 1.0, 0.0)
    bias = bias_ref[...].T * first
    rate = rate_ref[...].T * first
    for ch in range(16):
        at = slice(ch * 32, ch * 32 + 32)
        misc = beta
        if ch > 0:
            misc = jnp.broadcast_to(rate[:, ch : ch + 1], (32, 128))
        if ch == 1:
            misc = jnp.where(lane == 97, rate[:, 0:1], misc)
        mixed_ref[at, :] = jnp.where(
            lane < 32,
            query[at],
            jnp.where(lane < 64, key[at], jnp.where(lane < 96, gate[at] + bias[:, ch : ch + 1], misc)),
        )
    value = lax.dot_general(value_ref[...], across_four, NT, preferred_element_type=F32)
    wide = lanes((256, 128))
    mixed_ref[512:768, :] = jnp.where(
        wide < 32,
        value[0:256],
        jnp.where(wide < 64, value[256:512], jnp.where(wide < 96, value[512:768], value[768:1024])),
    )
    for slot in range(32):
        out_ref[slot] = mixed_ref[pl.ds(heads_ref[slot], 24, stride=32), :]


def spread(array, base):
    index = jnp.broadcast_to(lanes((1, 128)) // 32 + base, array.shape)
    return jnp.take_along_axis(array, index, axis=1)


def steps_kernel(arrived_ref, packed_ref, out_ref, state_ref, turned_ref, update_ref, result_ref, scale_ref):
    clip_norm = math.sqrt(DK * DV)
    steps = 4
    lane = lanes((128, 128))
    lane1 = lanes((1, 128))
    mixed = []
    for r in range(8):
        total = arrived_ref[4 * r, 0:16, :]
        for c in range(1, 4):
            total = total + arrived_ref[4 * r + c, 0:16, :]
        mixed.append(total)
    mixed = jnp.concatenate(mixed, axis=0)
    below = pltpu.roll(mixed, 127, 0)
    channel = rows_of((128, 1)) % 16
    rate = jnp.where(channel == 0, below[:, 97:98], mixed[:, 96:97])
    soft = jnp.maximum(mixed, 0.0) + jnp.log1p(jnp.exp(-jnp.abs(mixed)))
    alpha = jnp.exp(-rate * soft)
    key_size = jnp.sum(mixed * mixed, axis=0, keepdims=True)
    inverse = 1.0 / jnp.sqrt(key_size + EPSILON)
    scaled = mixed * jnp.where(lane1 < 32, DK ** (-0.5), inverse)
    cross = jnp.sum(scaled * pltpu.roll(scaled, 96, 1), axis=0, keepdims=True)
    prepared = jnp.where(lane < 64, scaled, alpha)
    write = 1.0 / (1.0 + jnp.exp(-mixed[0:1, :]))

    row8 = rows_of((8, 128))
    lane8 = lanes((8, 128))
    where_tok = (row8 // 2) * 8 + (row8 % 2) * 4 + lane8 // 32
    write8 = jnp.take_along_axis(jnp.broadcast_to(write, (8, 128)), where_tok + 96, axis=1)
    cross8 = jnp.take_along_axis(jnp.broadcast_to(cross, (8, 128)), where_tok, axis=1)

    values = []
    for c in range(4):
        total = arrived_ref[c, 16:24, :]
        for r in range(1, 8):
            total = total + arrived_ref[4 * r + c, 16:24, :]
        values.append(total)
    turned_ref[:, 0:32] = jnp.concatenate(values, axis=0).T
    turned_ref[:, 32:128] = jnp.zeros((128, 96), F32)
    value_rows = [jnp.zeros((8, 128), F32) for _ in range(4)]
    for lo in range(4):
        for octet in range(4):
            part = turned_ref[pl.ds(octet * 32 + lo, 8, stride=4), :]
            target = lo * 32 + octet * 8
            for c in range(4):
                moved = pltpu.roll(part, (target - c * 8) % 128, 1)
                value_rows[c] = jnp.where((lane8 >= target) & (lane8 < target + 8), moved, value_rows[c])

    for hi in range(2):
        for c in range(4):
            for r in range(8):
                upper = packed_ref[4 * r + c, hi * 16 : hi * 16 + 16, :].astype(F32)
                rest = packed_ref[4 * r + c, 32 + hi * 16 : 48 + hi * 16, :].astype(F32)
                state_ref[hi * 4 + c, r * 16 : r * 16 + 16, :] = upper + rest

    for hi in range(2):
        factor = None
        for t in range(steps):
            at = t * 2 + hi
            tok = t * 8 + hi * 4
            alpha_now = spread(prepared, 64 + tok)
            if factor is not None:
                alpha_now = alpha_now * factor
            key_now = spread(prepared, 32 + tok)
            query_now = spread(prepared, tok)
            write_now = write8[at : at + 1]
            cross_now = cross8[at : at + 1] * write_now
            squares = jnp.zeros((1, 128), F32)
            early = []
            for c in range(4):
                decayed = alpha_now * state_ref[hi * 4 + c]
                read = jnp.sum(key_now * decayed, axis=0, keepdims=True)
                probe = jnp.sum(query_now * decayed, axis=0, keepdims=True)
                residue = value_rows[c][at : at + 1] - read
                updated = decayed + key_now * (write_now * residue)
                state_ref[hi * 4 + c] = updated
                squares = squares + jnp.sum(updated * updated, axis=0, keepdims=True)
                update_ref[c, at : at + 1, :] = residue
                early.append(probe + cross_now * residue)
            norm = jnp.zeros((1, 128), F32)
            for lo in range(4):
                inside = lane1 // 32 == lo
                whole = jnp.sum(jnp.where(inside, squares, 0.0), axis=1, keepdims=True)
                norm = jnp.where(inside, whole, norm)
            factor = 1.0 / jnp.maximum(1.0, jnp.sqrt(norm) / clip_norm)
            scale_ref[at : at + 1, :] = factor
            for c in range(4):
                result_ref[c, at : at + 1, :] = early[c] * factor

    combined = jnp.zeros((128, 128), F32)
    for hi in range(2):
        carry = None
        for t in reversed(range(steps)):
            at = t * 2 + hi
            tok = t * 8 + hi * 4
            factor = scale_ref[at : at + 1, :]
            gain = spread(prepared, 32 + tok) * (write8[at : at + 1] * factor)
            decay = spread(prepared, 64 + tok) * factor
            if carry is not None:
                gain = gain * carry
                decay = decay * carry
            carry = decay
            combined = jnp.where(lane % 32 == at, gain, combined)
        combined = jnp.where(lane % 32 == 8 + hi, carry, combined)
    for r in range(8):
        upper = combined[16 * r : 16 * r + 8]
        lower = pltpu.roll(combined[16 * r + 8 : 16 * r + 16], 16, 1)
        both = jnp.where(lane8 % 32 < 16, upper, lower)
        for c in range(4):
            out_ref[4 * r + c, 0:8, :] = update_ref[c]
            out_ref[4 * r + c, 8:16, :] = result_ref[c]
            out_ref[4 * r + c, 16:24, :] = both


def finish_kernel(heads_ref, arrived_ref, state_ref, readout_ref, final_ref, update_ref, gain_ref):
    heads = state_ref.shape[3]
    slot = rows_of((heads, heads))
    head = lanes((heads, heads))
    order = jnp.zeros((heads, heads), F32)
    for s in range(heads):
        order = jnp.where((slot == s) & (head == heads_ref[s]), 1.0, order)
    order = order.astype(BF16)
    for at in range(8):
        t, hi = divmod(at, 2)
        update_ref[at] = arrived_ref[pl.ds(at, heads, stride=24), :].T
        gain_ref[at] = arrived_ref[pl.ds(16 + at, heads, stride=24), :].T
        result = arrived_ref[pl.ds(8 + at, heads, stride=24), :].astype(BF16)
        turned = lax.dot_general(result, order, TN, preferred_element_type=F32).astype(BF16)
        for lo in range(4):
            readout_ref[hi * 4 + lo, t] = turned[lo * 32 : lo * 32 + 32]
    for hi in range(2):
        for lo in range(4):
            updates = [update_ref[t * 2 + hi, lo * 32 : lo * 32 + 32, :] for t in range(4)]
            for i in range(16):
                i_hi, i_lo = divmod(i, 8)
                base = lo * 32 + i_hi * 16
                total = state_ref[hi * 4 + lo, i] * gain_ref[i_lo, base + 8 + hi : base + 9 + hi, :]
                for t in range(4):
                    at = base + t * 2 + hi
                    total = total + gain_ref[i_lo, at : at + 1, :] * updates[t]
                final_ref[hi * 4 + lo, i] = total


VMEM = pl.BlockSpec(memory_space=pltpu.VMEM)
SMEM = pl.BlockSpec(memory_space=pltpu.SMEM)
ANY = pl.BlockSpec(memory_space=pl.ANY)


def shape_of(shape, dtype):
    return jax.ShapeDtypeStruct(shape, dtype)


def shards(
    token_ids, slot_heads, embed_table, query_weight, key_weight, value_weight, decay_down, decay_up, decay_bias,
    decay_rate, beta_weight, init_state,
):
    groups = lax.axis_size("dp")
    ids = token_ids.T
    table = embed_table.T
    picked = pl.pallas_call(
        pick_kernel,
        out_shape=shape_of((groups, 32, 128), BF16),
        in_specs=[VMEM, VMEM],
        out_specs=VMEM,
        scratch_shapes=[pltpu.VMEM((4 * token_ids.shape[0], 1024), BF16)],
        interpret=INTERPRET,
        name="pick",
    )(ids, table)
    arrived = exchange(picked, "dp")
    packed = pl.pallas_call(
        pack_state_kernel,
        out_shape=shape_of((32, 96, 128), BF16),
        in_specs=[VMEM],
        out_specs=VMEM,
        scratch_shapes=[pltpu.VMEM((1024, 128), F32)],
        interpret=INTERPRET,
        name="pack_state",
    )(init_state)
    packed = pl.pallas_call(
        add_tokens_kernel,
        out_shape=shape_of((32, 96, 128), BF16),
        in_specs=[VMEM, ANY],
        out_specs=ANY,
        input_output_aliases={1: 0},
        scratch_shapes=[pltpu.VMEM((32, 128), BF16), pltpu.SemaphoreType.DMA((32,))],
        interpret=INTERPRET,
        name="add_tokens",
    )(arrived, packed)
    packed = exchange(packed, BOTH)
    projected = pl.pallas_call(
        project_kernel,
        out_shape=shape_of((32, 24, 128), F32),
        in_specs=[SMEM] + [VMEM] * 9,
        out_specs=VMEM,
        scratch_shapes=[pltpu.VMEM((768, 128), F32)],
        interpret=INTERPRET,
        name="project",
    )(
        slot_heads,
        packed,
        query_weight.transpose(1, 2, 0).reshape(512, -1),
        key_weight.transpose(1, 2, 0).reshape(512, -1),
        value_weight.transpose(1, 2, 0).reshape(1024, -1),
        decay_down,
        decay_up.transpose(1, 2, 0).reshape(512, -1),
        decay_bias,
        decay_rate,
        beta_weight.T,
    )
    projected = exchange(projected, BOTH)
    stepped = pl.pallas_call(
        steps_kernel,
        out_shape=shape_of((32, 24, 128), F32),
        in_specs=[VMEM, VMEM],
        out_specs=VMEM,
        scratch_shapes=[
            pltpu.VMEM((8, 128, 128), F32),
            pltpu.VMEM((128, 128), F32),
            pltpu.VMEM((4, 8, 128), F32),
            pltpu.VMEM((4, 8, 128), F32),
            pltpu.VMEM((8, 128), F32),
        ],
        interpret=INTERPRET,
        name="steps",
    )(projected, packed)
    stepped = exchange(stepped, BOTH)
    readout, final_state = pl.pallas_call(
        finish_kernel,
        out_shape=(shape_of((8, 4, 32, 32), BF16), shape_of(init_state.shape, F32)),
        in_specs=[SMEM, VMEM, VMEM],
        out_specs=(VMEM, VMEM),
        scratch_shapes=[pltpu.VMEM((8, 128, 32), F32), pltpu.VMEM((8, 128, 32), F32)],
        interpret=INTERPRET,
        name="finish",
    )(slot_heads, stepped.reshape(768, 128), init_state)
    return (readout, final_state)


def solution(mesh):
    in_specs = (
        P(),
        P(),
        P("dp", ("row", "col")),
        P("col", "row", None),
        P("col", "row", None),
        P("row", "col", None),
        P("col", None),
        P(None, "row", None),
        P("row", None),
        P("row", None),
        P("col", None),
        P("dp", "row", "col", None),
    )
    out_specs = (P("dp", None, "col", None), P("dp", "row", "col", None))
    return jax.shard_map(shards, mesh=mesh, in_specs=in_specs, out_specs=out_specs, check_vma=False)
```

time: 211 us -> 110 us (0.52)
  the two profiles are of different devices: /device:TPU:2 before, /device:TPU:8 now
where the time goes in v1:
time: 110 us
  blocking collectives  71.9 us (65%)
  Pallas kernels  20.5 us (19%)
  starting transfers between devices  10.4 us (9%)
  waiting for transfers between devices  5.46 us (5%)
    all_to_all x3, blocking collectives, exchange(): return lax.all_to_all(array, axis, split_axis=0, concat_axis=0, tiled=True)  71.9 us
    all_to_all x1, starting transfers between devices, exchange(): return lax.all_to_all(array, axis, split_axis=0, concat_axis=0, tiled=True)  10.4 us
    all_to_all x1, waiting for transfers between devices, exchange(): return lax.all_to_all(array, axis, split_axis=0, concat_axis=0, tiled=True)  5.46 us
    pallas_call x1, Pallas kernels, shards(): pl.pallas_call(finish_kernel, out_shape=(shape_of((8, 4, 32, 32), BF16),...  4.17 us
    pallas_call x1, Pallas kernels, shards(): pl.pallas_call(project_kernel, out_shape=shape_of((32, 24, 128), F32), in...  3.93 us
    pallas_call x1, Pallas kernels, shards(): pl.pallas_call(steps_kernel, out_shape=shape_of((32, 24, 128), F32), in_s...  3.76 us
    pallas_call x1, Pallas kernels, shards(): pl.pallas_call(pick_kernel, out_shape=shape_of((groups, 32, 128), BF16),...  3.56 us
    pallas_call x1, Pallas kernels, shards(): pl.pallas_call(pack_state_kernel, out_shape=shape_of((32, 96, 128), BF16)...  3.19 us
  transfers between devices with their start and end apart: 1, of which 1 were waited for; matrix products, arithmetic and copies ran while one was open for 0% of the time, Pallas kernels for 3%

profile of v1, /device:TPU:8, one launch (start us, length us, event | category | flops | bytes accessed | tf_op | source)
XLA Modules:
  0.0 109.6 jit_solution(14193847782061123208)
XLA Ops:
  0.6 3.6 %pick.1 = bf16[16,32,128]{2,1,0:T(8,128)(2,1)} custom-call(s32[4,128]{1,0:T(4,128)} %bitcast.23, bf16[72,5120]{1,0:T(8,128)(2,1)} %bitcast.18), custom_call_target="tpu_custom_call" | custom-call | tf_op jit(solution)/shard_map/pick/pallas_call | solution.py:323
  4.2 10.4 %all-to-all-start = ((bf16[16,32,128]{2,1,0:T(8,128)(2,1)}), bf16[16,32,128]{2,1,0:T(8,128)(2,1)S(1)}, u32[]{:S(2)}, u32[]{:S(2)}) async-start(bf16[16,32,128]{2,1,0:T(8,128)(2,1)} %pick.1), calls=%async_computation | async-start | bytes 262144 | tf_op jit(solution)/shard_map/all_to_all | solution.py:32
  14.6 3.2 %pack_state.1.packed_ref = bf16[32,96,128]{2,1,0:T(8,128)(2,1)} custom-call(f32[8,16,32,32]{3,2,1,0:T(8,128)} %state_ref.3), custom_call_target="tpu_custom_call" | custom-call | tf_op jit(solution)/shard_map/pack_state/pallas_call | solution.py:333
  17.8 5.5 %all-to-all-done.arrived_ref = bf16[16,32,128]{2,1,0:T(8,128)(2,1)S(1)} async-done(((bf16[16,32,128]{2,1,0:T(8,128)(2,1)}), bf16[16,32,128]{2,1,0:T(8,128)(2,1)S(1)}, u32[]{:S(2)}, u32[]{:S(2)}) %all-to-all-start) | async-done | bytes 131104 | tf_op jit(solution)/shard_map/all_to_all | solution.py:32
  23.3 0.0 copy-start
  23.3 0.7 copy-done
  23.9 1.9 %add_tokens.1 = bf16[32,96,128]{2,1,0:T(8,128)(2,1)} custom-call(bf16[16,32,128]{2,1,0:T(8,128)(2,1)} %copy-done, bf16[32,96,128]{2,1,0:T(8,128)(2,1)} %pack_state.1.packed_ref), custom_call_target="tpu_custom_call", output_to_operand_aliasing={{}: (1, {})} | custom-call | tf_op jit(solution)/shard_map/add_tokens/pallas_call | solution.py:342
  25.8 32.7 %all_to_all.20.arrived_ref.packed_ref = bf16[32,96,128]{2,1,0:T(8,128)(2,1)} all-to-all(bf16[32,96,128]{2,1,0:T(8,128)(2,1)} %add_tokens.1), channel_id=1, replica_groups=mesh['dp'=16,'row'=8,'col'=4] {'row','col'}, dimensions={0} | all-to-all | bytes 1572864 | tf_op jit(solution)/shard_map/all_to_all | solution.py:32
  58.6 3.9 %project.1 = f32[32,24,128]{2,1,0:T(8,128)} custom-call(s32[32]{0:T(128)} %heads_ref.3, bf16[32,96,128]{2,1,0:T(8,128)(2,1)} %all_to_all.20.arrived_ref.packed_ref, bf16[512,576]{1,0:T(8,128)(2,1)} %bitcast.19, bf16[512,576]{1,0:T(8,128)(2,1)} %bitcast.20, bf16[1024,288]{1,0:T(8,128)(2,1)} %bitcast.17, bf16[576,128]{1,0:T(8,128)(2,1)} %down_ref.1, ...), custom_call_target="tpu_custom_call" | custom-call | tf_op jit(solution)/shard_map/project/pallas_call | solution.py:353
  62.5 20.4 %all_to_all.21.arrived_ref = f32[32,24,128]{2,1,0:T(8,128)} all-to-all(f32[32,24,128]{2,1,0:T(8,128)} %project.1), channel_id=1, replica_groups=mesh['dp'=16,'row'=8,'col'=4] {'row','col'}, dimensions={0} | all-to-all | bytes 786432 | tf_op jit(solution)/shard_map/all_to_all | solution.py:32
  82.9 3.8 %steps.1 = f32[32,24,128]{2,1,0:T(8,128)} custom-call(f32[32,24,128]{2,1,0:T(8,128)} %all_to_all.21.arrived_ref, bf16[32,96,128]{2,1,0:T(8,128)(2,1)} %all_to_all.20.arrived_ref.packed_ref), custom_call_target="tpu_custom_call" | custom-call | tf_op jit(solution)/shard_map/steps/pallas_call | solution.py:374
  86.7 18.7 %all_to_all.22 = f32[32,24,128]{2,1,0:T(8,128)} all-to-all(f32[32,24,128]{2,1,0:T(8,128)} %steps.1), channel_id=1, replica_groups=mesh['dp'=16,'row'=8,'col'=4] {'row','col'}, dimensions={0} | all-to-all | bytes 786432 | tf_op jit(solution)/shard_map/all_to_all | solution.py:32
  105.4 4.2 %finish.1 = (bf16[8,4,32,32]{3,2,1,0:T(8,128)(2,1)}, f32[8,16,32,32]{3,2,1,0:T(8,128)}) custom-call(s32[32]{0:T(128)} %heads_ref.3, f32[768,128]{1,0:T(8,128)} %bitcast.16, f32[8,16,32,32]{3,2,1,0:T(8,128)} %state_ref.3), custom_call_target="tpu_custom_call" | custom-call | tf_op jit(solution)/shard_map/finish/pallas_call | solution.py:390
Async XLA Ops:
  4.2 19.1 %all-to-all-start = ((bf16[16,32,128]{2,1,0:T(8,128)(2,1)}), bf16[16,32,128]{2,1,0:T(8,128)(2,1)S(1)}, u32[]{:S(2)}, u32[]{:S(2)}) async-start(bf16[16,32,128]{2,1,0:T(8,128)(2,1)} %pick.1), calls=%async_computation | async-start | bytes 262144 | tf_op jit(solution)/shard_map/all_to_all | solution.py:32
  23.3 0.7 copy-start

commit v2 on v1

--- a/solution.py
+++ b/solution.py
@@ -28,8 +28,15 @@
     return lax.broadcasted_iota(jnp.int32, shape, len(shape) - 2)
 
 
-def exchange(array, axis):
-    return lax.all_to_all(array, axis, split_axis=0, concat_axis=0, tiled=True)
+def exchange(array, axis, shape=None):
+    array = lax.all_to_all(array, axis, split_axis=0, concat_axis=0, tiled=True)
+    if shape is not None:
+        array = array.reshape(shape)
+    return kept(array)
+
+
+def kept(array):
+    return array if INTERPRET else pltpu.with_memory_space_constraint(array, pltpu.VMEM)
 
 
 def pick_kernel(ids_ref, table_ref, out_ref, onehot_ref):
@@ -60,32 +67,28 @@
             out_ref[:, (t - 1) * 8 : (t + 1) * 8, :] = pair.astype(BF16)
 
 
-def pack_state_kernel(state_ref, out_ref, turned_ref):
+def pack_state_kernel(state_ref, early_ref, late_ref, turned_ref):
     heads = state_ref.shape[3]
     for hi in range(2):
         for i in range(16):
             block = state_ref[hi * 4 : hi * 4 + 4, i].reshape(128, heads)
             turned_ref[pl.ds(hi * 16 + i, heads, stride=32), :] = block.T
     whole = turned_ref[...].reshape(heads, 32, 128)
-    upper = whole.astype(BF16)
-    out_ref[:, 0:32, :] = upper
-    out_ref[:, 32:64, :] = (whole - upper.astype(F32)).astype(BF16)
-
-
-def add_tokens_kernel(arrived_ref, packed_ref, out_ref, own_ref, sems):
-    del packed_ref
+    first = whole[:, 0:16]
+    upper = first.astype(BF16)
+    early_ref[:, 0:16, :] = upper
+    early_ref[:, 16:32, :] = (first - upper.astype(F32)).astype(BF16)
+    late_ref[...] = whole[:, 16:32]
+
+
+def add_tokens_kernel(arrived_ref, early_ref, out_ref):
     total = arrived_ref[0].astype(F32)
     for k in range(1, arrived_ref.shape[0]):
         total = total + arrived_ref[k].astype(F32)
-    own_ref[...] = total.astype(BF16)
-    peers = out_ref.shape[0]
-    copies = [
-        pltpu.make_async_copy(own_ref, out_ref.at[p, 64:96, :], sems.at[p]) for p in range(peers)
-    ]
-    for copy in copies:
-        copy.start()
-    for copy in copies:
-        copy.wait()
+    own = total.astype(BF16)
+    out_ref[:, 0:32, :] = early_ref[...]
+    for p in range(out_ref.shape[0]):
+        out_ref[p, 32:64, :] = own
 
 
 def side_by_side(blocks, width):
@@ -104,14 +107,14 @@
 
 def project_kernel(
     heads_ref, arrived_ref, query_ref, key_ref, value_ref, down_ref, up_ref, bias_ref, rate_ref, beta_ref,
-    out_ref, mixed_ref,
+    late_ref, out_ref, mixed_ref,
 ):
     col = lax.axis_index("col")
     row = lax.axis_index("row")
     width = query_ref.shape[1] // 8
 
     def features(first, count):
-        blocks = [arrived_ref[first + k, 64:96, :].astype(F32) for k in range(count)]
+        blocks = [arrived_ref[first + k, 32:64, :].astype(F32) for k in range(count)]
         return side_by_side(blocks, width)[:, : count * width].astype(BF16)
 
     own = features(col * 8, 8)
@@ -154,7 +157,8 @@
         jnp.where(wide < 64, value[256:512], jnp.where(wide < 96, value[512:768], value[768:1024])),
     )
     for slot in range(32):
-        out_ref[slot] = mixed_ref[pl.ds(heads_ref[slot], 24, stride=32), :]
+        out_ref[slot, 0:24, :] = mixed_ref[pl.ds(heads_ref[slot], 24, stride=32), :]
+    out_ref[:, 24:40, :] = late_ref[...]
 
 
 def spread(array, base):
@@ -209,12 +213,12 @@
                 moved = pltpu.roll(part, (target - c * 8) % 128, 1)
                 value_rows[c] = jnp.where((lane8 >= target) & (lane8 < target + 8), moved, value_rows[c])
 
-    for hi in range(2):
-        for c in range(4):
-            for r in range(8):
-                upper = packed_ref[4 * r + c, hi * 16 : hi * 16 + 16, :].astype(F32)
-                rest = packed_ref[4 * r + c, 32 + hi * 16 : 48 + hi * 16, :].astype(F32)
-                state_ref[hi * 4 + c, r * 16 : r * 16 + 16, :] = upper + rest
+    for c in range(4):
+        for r in range(8):
+            at = slice(r * 16, r * 16 + 16)
+            upper = packed_ref[4 * r + c, 0:16, :].astype(F32)
+            state_ref[c, at, :] = upper + packed_ref[4 * r + c, 16:32, :].astype(F32)
+            state_ref[4 + c, at, :] = arrived_ref[4 * r + c, 24:40, :]
 
     for hi in range(2):
         factor = None
@@ -306,11 +310,14 @@
 
 VMEM = pl.BlockSpec(memory_space=pltpu.VMEM)
 SMEM = pl.BlockSpec(memory_space=pltpu.SMEM)
-ANY = pl.BlockSpec(memory_space=pl.ANY)
 
 
 def shape_of(shape, dtype):
     return jax.ShapeDtypeStruct(shape, dtype)
+
+
+def on_chip(shape, dtype):
+    return shape_of(shape, dtype) if INTERPRET else pltpu.VMEM(shape, dtype)
 
 
 def shards(
@@ -322,7 +329,7 @@
     table = embed_table.T
     picked = pl.pallas_call(
         pick_kernel,
-        out_shape=shape_of((groups, 32, 128), BF16),
+        out_shape=on_chip((groups, 32, 128), BF16),
         in_specs=[VMEM, VMEM],
         out_specs=VMEM,
         scratch_shapes=[pltpu.VMEM((4 * token_ids.shape[0], 1024), BF16)],
@@ -330,30 +337,28 @@
         name="pick",
     )(ids, table)
     arrived = exchange(picked, "dp")
-    packed = pl.pallas_call(
+    early, late = pl.pallas_call(
         pack_state_kernel,
-        out_shape=shape_of((32, 96, 128), BF16),
+        out_shape=(on_chip((32, 32, 128), BF16), on_chip((32, 16, 128), F32)),
         in_specs=[VMEM],
-        out_specs=VMEM,
+        out_specs=(VMEM, VMEM),
         scratch_shapes=[pltpu.VMEM((1024, 128), F32)],
         interpret=INTERPRET,
         name="pack_state",
     )(init_state)
     packed = pl.pallas_call(
         add_tokens_kernel,
-        out_shape=shape_of((32, 96, 128), BF16),
-        in_specs=[VMEM, ANY],
-        out_specs=ANY,
-        input_output_aliases={1: 0},
-        scratch_shapes=[pltpu.VMEM((32, 128), BF16), pltpu.SemaphoreType.DMA((32,))],
+        out_shape=on_chip((32, 64, 128), BF16),
+        in_specs=[VMEM, VMEM],
+        out_specs=VMEM,
         interpret=INTERPRET,
         name="add_tokens",
-    )(arrived, packed)
+    )(arrived, kept(early))
     packed = exchange(packed, BOTH)
     projected = pl.pallas_call(
         project_kernel,
-        out_shape=shape_of((32, 24, 128), F32),
-        in_specs=[SMEM] + [VMEM] * 9,
+        out_shape=on_chip((32, 40, 128), F32),
+        in_specs=[SMEM] + [VMEM] * 10,
         out_specs=VMEM,
         scratch_shapes=[pltpu.VMEM((768, 128), F32)],
         interpret=INTERPRET,
@@ -369,11 +374,12 @@
         decay_bias,
         decay_rate,
         beta_weight.T,
+        kept(late),
     )
     projected = exchange(projected, BOTH)
     stepped = pl.pallas_call(
         steps_kernel,
-        out_shape=shape_of((32, 24, 128), F32),
+        out_shape=on_chip((32, 24, 128), F32),
         in_specs=[VMEM, VMEM],
         out_specs=VMEM,
         scratch_shapes=[
@@ -386,7 +392,7 @@
         interpret=INTERPRET,
         name="steps",
     )(projected, packed)
-    stepped = exchange(stepped, BOTH)
+    stepped = exchange(stepped, BOTH, (768, 128))
     readout, final_state = pl.pallas_call(
         finish_kernel,
         out_shape=(shape_of((8, 4, 32, 32), BF16), shape_of(init_state.shape, F32)),
@@ -395,7 +401,7 @@
         scratch_shapes=[pltpu.VMEM((8, 128, 32), F32), pltpu.VMEM((8, 128, 32), F32)],
         interpret=INTERPRET,
         name="finish",
-    )(slot_heads, stepped.reshape(768, 128), init_state)
+    )(slot_heads, stepped, init_state)
     return (readout, final_state)
 
 

time: 110 us -> 104 us (0.945)
  Pallas kernels: 20.5 us -> 14.7 us
    pallas_call x5, Pallas kernels: 16.4 us -> 10.6 us  [the longest x1 3.56 us: shards(): pl.pallas_call(pick_kernel, out_shape=on_chip((groups, 32, 128), BF16), i...]
  transfers between devices with their start and end apart: 1 -> 1, of which waited for: 1 -> 1; matrix products, arithmetic and copies ran while one was open for 0% -> 0% of each run, Pallas kernels for 3% -> 2%
where the time goes in v2:
time: 104 us; the launch traced here: 103 us
  blocking collectives  71.2 us (68%)
  Pallas kernels  14.7 us (14%)
  starting transfers between devices  10.4 us (10%)
  waiting for transfers between devices  6.34 us (6%)
    all_to_all x3, blocking collectives, exchange(): array = lax.all_to_all(array, axis, split_axis=0, concat_axis=0, tiled=True)  71.2 us
    all_to_all x1, starting transfers between devices, exchange(): array = lax.all_to_all(array, axis, split_axis=0, concat_axis=0, tiled=True)  10.4 us
    all_to_all x1, waiting for transfers between devices, exchange(): array = lax.all_to_all(array, axis, split_axis=0, concat_axis=0, tiled=True)  6.34 us
    pallas_call x1, Pallas kernels, shards(): pl.pallas_call(finish_kernel, out_shape=(shape_of((8, 4, 32, 32), BF16),...  4.03 us
    pallas_call x1, Pallas kernels, shards(): pl.pallas_call(pick_kernel, out_shape=on_chip((groups, 32, 128), BF16), i...  3.56 us
    pallas_call x1, Pallas kernels, shards(): pl.pallas_call(project_kernel, out_shape=on_chip((32, 40, 128), F32), in_...  2.96 us
    pallas_call x1, Pallas kernels, shards(): pl.pallas_call(pack_state_kernel, out_shape=(on_chip((32, 32, 128), BF16)...  2.3 us
  transfers between devices with their start and end apart: 1, of which 1 were waited for; matrix products, arithmetic and copies ran while one was open for 0% of the time, Pallas kernels for 2%

profile of v2, /device:TPU:8, one launch (start us, length us, event | category | flops | bytes accessed | tf_op | source)
XLA Modules:
  0.0 103.3 jit_solution(15803637517360159550)
XLA Ops:
  0.6 3.6 %pick.1 = bf16[16,32,128]{2,1,0:T(8,128)(2,1)} custom-call(s32[4,128]{1,0:T(4,128)} %bitcast.23, bf16[72,5120]{1,0:T(8,128)(2,1)} %bitcast.18), custom_call_target="tpu_custom_call" | custom-call | tf_op jit(solution)/shard_map/pick/pallas_call | solution.py:330
  4.2 10.4 %all-to-all-start = ((bf16[16,32,128]{2,1,0:T(8,128)(2,1)}), bf16[16,32,128]{2,1,0:T(8,128)(2,1)S(1)}, u32[]{:S(2)}, u32[]{:S(2)}) async-start(bf16[16,32,128]{2,1,0:T(8,128)(2,1)} %pick.1), calls=%async_computation | async-start | bytes 262144 | tf_op jit(solution)/shard_map/all_to_all | solution.py:32
  14.6 2.3 %pack_state.1 = (bf16[32,32,128]{2,1,0:T(8,128)(2,1)S(1)}, f32[32,16,128]{2,1,0:T(8,128)S(1)}) custom-call(f32[8,16,32,32]{3,2,1,0:T(8,128)} %state_ref.3), custom_call_target="tpu_custom_call" | custom-call | tf_op jit(solution)/shard_map/pack_state/pallas_call | solution.py:340
  16.9 6.3 %all-to-all-done.arrived_ref = bf16[16,32,128]{2,1,0:T(8,128)(2,1)S(1)} async-done(((bf16[16,32,128]{2,1,0:T(8,128)(2,1)}), bf16[16,32,128]{2,1,0:T(8,128)(2,1)S(1)}, u32[]{:S(2)}, u32[]{:S(2)}) %all-to-all-start) | async-done | bytes 131104 | tf_op jit(solution)/shard_map/all_to_all | solution.py:32
  23.3 0.1 add_tokens.1
  23.3 27.7 %all_to_all.20.arrived_ref.packed_ref = bf16[32,64,128]{2,1,0:T(8,128)(2,1)S(1)} all-to-all(bf16[32,64,128]{2,1,0:T(8,128)(2,1)S(1)} %add_tokens.1), channel_id=1, replica_groups=mesh['dp'=16,'row'=8,'col'=4] {'row','col'}, dimensions={0} | all-to-all | bytes 1048576 | tf_op jit(solution)/shard_map/all_to_all | solution.py:32
  51.0 3.0 %project.1 = f32[32,40,128]{2,1,0:T(8,128)S(1)} custom-call(s32[32]{0:T(128)} %heads_ref.3, bf16[32,64,128]{2,1,0:T(8,128)(2,1)S(1)} %all_to_all.20.arrived_ref.packed_ref, bf16[512,576]{1,0:T(8,128)(2,1)} %bitcast.19, bf16[512,576]{1,0:T(8,128)(2,1)} %bitcast.20, bf16[1024,288]{1,0:T(8,128)(2,1)} %bitcast.17, bf16[576,128]{1,0:T(8,128)(2,1)} %down_ref.1, ...), custom_call_target="tpu_custom_call" | custom-call | tf_op jit(solution)/shard_map/project/pallas_call | solution.py:358
  54.0 24.6 %all_to_all.21.arrived_ref = f32[32,40,128]{2,1,0:T(8,128)S(1)} all-to-all(f32[32,40,128]{2,1,0:T(8,128)S(1)} %project.1), channel_id=1, replica_groups=mesh['dp'=16,'row'=8,'col'=4] {'row','col'}, dimensions={0} | all-to-all | bytes 1310720 | tf_op jit(solution)/shard_map/all_to_all | solution.py:32
  78.5 1.8 %steps.1 = f32[32,24,128]{2,1,0:T(8,128)S(1)} custom-call(f32[32,40,128]{2,1,0:T(8,128)S(1)} %all_to_all.21.arrived_ref, bf16[32,64,128]{2,1,0:T(8,128)(2,1)S(1)} %all_to_all.20.arrived_ref.packed_ref), custom_call_target="tpu_custom_call" | custom-call | tf_op jit(solution)/shard_map/steps/pallas_call | solution.py:380
  80.3 18.9 %all_to_all.22 = f32[32,24,128]{2,1,0:T(8,128)S(1)} all-to-all(f32[32,24,128]{2,1,0:T(8,128)S(1)} %steps.1), channel_id=1, replica_groups=mesh['dp'=16,'row'=8,'col'=4] {'row','col'}, dimensions={0} | all-to-all | bytes 786432 | tf_op jit(solution)/shard_map/all_to_all | solution.py:32
  99.2 4.0 %finish.1 = (bf16[8,4,32,32]{3,2,1,0:T(8,128)(2,1)}, f32[8,16,32,32]{3,2,1,0:T(8,128)}) custom-call(s32[32]{0:T(128)} %heads_ref.3, f32[768,128]{1,0:T(8,128)S(1)} %bitcast.16, f32[8,16,32,32]{3,2,1,0:T(8,128)} %state_ref.3), custom_call_target="tpu_custom_call" | custom-call | tf_op jit(solution)/shard_map/finish/pallas_call | solution.py:396
Async XLA Ops:
  4.2 19.1 %all-to-all-start = ((bf16[16,32,128]{2,1,0:T(8,128)(2,1)}), bf16[16,32,128]{2,1,0:T(8,128)(2,1)S(1)}, u32[]{:S(2)}, u32[]{:S(2)}) async-start(bf16[16,32,128]{2,1,0:T(8,128)(2,1)} %pick.1), calls=%async_computation | async-start | bytes 262144 | tf_op jit(solution)/shard_map/all_to_all | solution.py:32

commit v3 on v2

--- a/solution.py
+++ b/solution.py
@@ -44,26 +44,34 @@
     feats, vocab = table_ref.shape
     groups = out_ref.shape[0]
     start = lax.axis_index("dp") * vocab
-    chunk = onehot_ref.shape[1]
-    columns = jnp.broadcast_to((ids_ref[...] - start).astype(F32)[:, None, :], (steps, 8, streams))
-    columns = [columns[t].T.astype(jnp.int32)[:, 0:1] for t in range(steps)]
+    local = jnp.broadcast_to((ids_ref[...] - start)[:, None, :], (steps, 8, streams))
+    block_of = (local >> 7).astype(F32)
+    place_of = (local & 127).astype(F32)
+    blocks, places = [], []
+    for t in range(steps):
+        blocks.append(jnp.broadcast_to(block_of[t].T[:, 0:1], (streams, 128)))
+        places.append(place_of[t].T[:, 0:1])
+    lane = lanes((streams, 128)).astype(F32)
+    blocks = jnp.concatenate(blocks, axis=0).astype(BF16)
+    hits = jnp.concatenate([jnp.where(lane == place, 1.0, 0.0) for place in places], axis=0).astype(BF16)
+    none = jnp.zeros_like(hits)
+    width = onehot_ref.shape[1]
     total = None
-    for part in range(vocab // chunk):
-        position = lanes((streams, chunk)) + part * chunk
-        for t in range(steps):
-            hit = columns[t] == position
-            onehot_ref[t * streams : (t + 1) * streams, :] = jnp.where(hit, 1.0, 0.0).astype(BF16)
+    for part in range(vocab // width):
+        for k in range(width // 128):
+            number = jnp.asarray(part * (width // 128) + k, BF16)
+            onehot_ref[:, k * 128 : (k + 1) * 128] = jnp.where(blocks == number, hits, none)
         found = lax.dot_general(
-            onehot_ref[...], table_ref[:, part * chunk : (part + 1) * chunk], NT, preferred_element_type=F32
+            onehot_ref[...], table_ref[:, part * width : (part + 1) * width], NT, preferred_element_type=F32
         )
         total = found if total is None else total + found
     wide = jnp.concatenate([total, jnp.zeros((total.shape[0], 128 - feats), F32)], axis=1)
     for t in range(steps):
         block = wide[t * streams : (t + 1) * streams].reshape(groups, 8, 128)
         if t % 2 == 0:
-            kept = block
+            held = block
         else:
-            pair = jnp.concatenate([kept, block], axis=1)
+            pair = jnp.concatenate([held, block], axis=1)
             out_ref[:, (t - 1) * 8 : (t + 1) * 8, :] = pair.astype(BF16)
 
 
@@ -279,8 +287,26 @@
             out_ref[4 * r + c, 16:24, :] = both
 
 
-def finish_kernel(heads_ref, arrived_ref, state_ref, readout_ref, final_ref, update_ref, gain_ref):
+def finish_kernel(heads_ref, arrived_ref, state_ref, readout_ref, final_ref, update_ref, gain_ref, last_ref, sems):
     heads = state_ref.shape[3]
+    for at in range(8):
+        update_ref[at] = arrived_ref[pl.ds(at, heads, stride=24), :].T
+        gain_ref[at] = arrived_ref[pl.ds(16 + at, heads, stride=24), :].T
+    copies = []
+    for hi in range(2):
+        for lo in range(4):
+            stream = hi * 4 + lo
+            updates = [update_ref[t * 2 + hi, lo * 32 : lo * 32 + 32, :] for t in range(4)]
+            for i in range(16):
+                i_hi, i_lo = divmod(i, 8)
+                base = lo * 32 + i_hi * 16
+                total = state_ref[stream, i] * gain_ref[i_lo, base + 8 + hi : base + 9 + hi, :]
+                for t in range(4):
+                    at = base + t * 2 + hi
+                    total = total + gain_ref[i_lo, at : at + 1, :] * updates[t]
+                last_ref[stream, i] = total
+            copies.append(pltpu.make_async_copy(last_ref.at[stream], final_ref.at[stream], sems.at[stream]))
+            copies[-1].start()
     slot = rows_of((heads, heads))
     head = lanes((heads, heads))
     order = jnp.zeros((heads, heads), F32)
@@ -289,27 +315,17 @@
     order = order.astype(BF16)
     for at in range(8):
         t, hi = divmod(at, 2)
-        update_ref[at] = arrived_ref[pl.ds(at, heads, stride=24), :].T
-        gain_ref[at] = arrived_ref[pl.ds(16 + at, heads, stride=24), :].T
         result = arrived_ref[pl.ds(8 + at, heads, stride=24), :].astype(BF16)
         turned = lax.dot_general(result, order, TN, preferred_element_type=F32).astype(BF16)
         for lo in range(4):
             readout_ref[hi * 4 + lo, t] = turned[lo * 32 : lo * 32 + 32]
-    for hi in range(2):
-        for lo in range(4):
-            updates = [update_ref[t * 2 + hi, lo * 32 : lo * 32 + 32, :] for t in range(4)]
-            for i in range(16):
-                i_hi, i_lo = divmod(i, 8)
-                base = lo * 32 + i_hi * 16
-                total = state_ref[hi * 4 + lo, i] * gain_ref[i_lo, base + 8 + hi : base + 9 + hi, :]
-                for t in range(4):
-                    at = base + t * 2 + hi
-                    total = total + gain_ref[i_lo, at : at + 1, :] * updates[t]
-                final_ref[hi * 4 + lo, i] = total
+    for copy in copies:
+        copy.wait()
 
 
 VMEM = pl.BlockSpec(memory_space=pltpu.VMEM)
 SMEM = pl.BlockSpec(memory_space=pltpu.SMEM)
+ANY = pl.BlockSpec(memory_space=pl.ANY)
 
 
 def shape_of(shape, dtype):
@@ -325,6 +341,7 @@
     decay_rate, beta_weight, init_state,
 ):
     groups = lax.axis_size("dp")
+    state = kept(init_state)
     ids = token_ids.T
     table = embed_table.T
     picked = pl.pallas_call(
@@ -334,6 +351,7 @@
         out_specs=VMEM,
         scratch_shapes=[pltpu.VMEM((4 * token_ids.shape[0], 1024), BF16)],
         interpret=INTERPRET,
+        compiler_params=pltpu.CompilerParams(vmem_limit_bytes=16 << 20),
         name="pick",
     )(ids, table)
     arrived = exchange(picked, "dp")
@@ -344,14 +362,16 @@
         out_specs=(VMEM, VMEM),
         scratch_shapes=[pltpu.VMEM((1024, 128), F32)],
         interpret=INTERPRET,
+        compiler_params=pltpu.CompilerParams(vmem_limit_bytes=16 << 20),
         name="pack_state",
-    )(init_state)
+    )(state)
     packed = pl.pallas_call(
         add_tokens_kernel,
         out_shape=on_chip((32, 64, 128), BF16),
         in_specs=[VMEM, VMEM],
         out_specs=VMEM,
         interpret=INTERPRET,
+        compiler_params=pltpu.CompilerParams(vmem_limit_bytes=16 << 20),
         name="add_tokens",
     )(arrived, kept(early))
     packed = exchange(packed, BOTH)
@@ -362,15 +382,16 @@
         out_specs=VMEM,
         scratch_shapes=[pltpu.VMEM((768, 128), F32)],
         interpret=INTERPRET,
+        compiler_params=pltpu.CompilerParams(vmem_limit_bytes=16 << 20),
         name="project",
     )(
         slot_heads,
         packed,
-        query_weight.transpose(1, 2, 0).reshape(512, -1),
-        key_weight.transpose(1, 2, 0).reshape(512, -1),
-        value_weight.transpose(1, 2, 0).reshape(1024, -1),
-        decay_down,
-        decay_up.transpose(1, 2, 0).reshape(512, -1),
+        kept(query_weight.transpose(1, 2, 0).reshape(512, -1)),
+        kept(key_weight.transpose(1, 2, 0).reshape(512, -1)),
+        kept(value_weight.transpose(1, 2, 0).reshape(1024, -1)),
+        kept(decay_down),
+        kept(decay_up.transpose(1, 2, 0).reshape(512, -1)),
         decay_bias,
         decay_rate,
         beta_weight.T,
@@ -390,6 +411,7 @@
             pltpu.VMEM((8, 128), F32),
         ],
         interpret=INTERPRET,
+        compiler_params=pltpu.CompilerParams(vmem_limit_bytes=16 << 20),
         name="steps",
     )(projected, packed)
     stepped = exchange(stepped, BOTH, (768, 128))
@@ -397,11 +419,17 @@
         finish_kernel,
         out_shape=(shape_of((8, 4, 32, 32), BF16), shape_of(init_state.shape, F32)),
         in_specs=[SMEM, VMEM, VMEM],
-        out_specs=(VMEM, VMEM),
-        scratch_shapes=[pltpu.VMEM((8, 128, 32), F32), pltpu.VMEM((8, 128, 32), F32)],
-        interpret=INTERPRET,
+        out_specs=(VMEM, ANY),
+        scratch_shapes=[
+            pltpu.VMEM((8, 128, 32), F32),
+            pltpu.VMEM((8, 128, 32), F32),
+            pltpu.VMEM((8, 16, 32, 32), F32),
+            pltpu.SemaphoreType.DMA((8,)),
+        ],
+        interpret=INTERPRET,
+        compiler_params=pltpu.CompilerParams(vmem_limit_bytes=16 << 20),
         name="finish",
-    )(slot_heads, stepped, init_state)
+    )(slot_heads, stepped, state)
     return (readout, final_state)
 
 

time: 104 us -> 104 us (level)
  Pallas kernels: 14.7 us -> 11 us
  local copies, waits for them, and re-layouts: 0 us -> 3.43 us
    unnamed x0 -> x26, local copies, waits for them, and re-layouts: none -> 3.43 us
    pallas_call x1, Pallas kernels: 2.3 us -> 0.71 us  [shards(): pl.pallas_call(pack_state_kernel, out_shape=(on_chip((32, 32, 128), BF16)...]
    pallas_call x1, Pallas kernels: 2.96 us -> 1.89 us  [shards(): pl.pallas_call(project_kernel, out_shape=on_chip((32, 40, 128), F32), in_...]
  transfers between devices with their start and end apart: 1 -> 1, of which waited for: 1 -> 1; matrix products, arithmetic and copies ran while one was open for 0% -> 0% of each run, Pallas kernels for 2% -> 1%
where the time goes in v3:
time: 104 us; the launch traced here: 103 us
  blocking collectives  71.3 us (69%)
  Pallas kernels  11 us (11%)
  starting transfers between devices  10.4 us (10%)
  waiting for transfers between devices  6.27 us (6%)
  local copies, waits for them, and re-layouts  3.43 us (3%)
    all_to_all x3, blocking collectives, exchange(): array = lax.all_to_all(array, axis, split_axis=0, concat_axis=0, tiled=True)  71.3 us
    all_to_all x1, starting transfers between devices, exchange(): array = lax.all_to_all(array, axis, split_axis=0, concat_axis=0, tiled=True)  10.4 us
    all_to_all x1, waiting for transfers between devices, exchange(): array = lax.all_to_all(array, axis, split_axis=0, concat_axis=0, tiled=True)  6.27 us
    pallas_call x1, Pallas kernels, shards(): pl.pallas_call(finish_kernel, out_shape=(shape_of((8, 4, 32, 32), BF16),...  3.46 us
    unnamed x26, local copies, waits for them, and re-layouts  3.43 us
    pallas_call x1, Pallas kernels, shards(): pl.pallas_call(pick_kernel, out_shape=on_chip((groups, 32, 128), BF16), i...  3.14 us
  transfers between devices with their start and end apart: 1, of which 1 were waited for; matrix products, arithmetic and copies ran while one was open for 0% of the time, Pallas kernels for 1%

profile of v3, /device:TPU:8, one launch (start us, length us, event | category | flops | bytes accessed | tf_op | source)
XLA Modules:
  0.0 103.2 jit_solution(7756800065766529842)
XLA Ops:
  0.6 0.0 copy-start.3
  0.6 1.1 %copy-done.3 = bf16[5120,72]{0,1:T(8,128)(2,1)S(1)} copy-done((bf16[5120,72]{0,1:T(8,128)(2,1)S(1)}, bf16[5120,72]{0,1:T(8,128)(2,1)}, u32[]{:S(2)}) %copy-start.3) | copy-done | bytes 737304
  1.7 0.7 copy-done.11
  2.4 3.1 %pick.1 = bf16[16,32,128]{2,1,0:T(8,128)(2,1)} custom-call(s32[4,128]{1,0:T(4,128)S(1)} %bitcast.23, bf16[72,5120]{1,0:T(8,128)(2,1)S(1)} %bitcast.18), custom_call_target="tpu_custom_call" | custom-call | tf_op jit(solution)/shard_map/pick/pallas_call | solution.py:347
  5.6 10.4 %all-to-all-start = ((bf16[16,32,128]{2,1,0:T(8,128)(2,1)}), bf16[16,32,128]{2,1,0:T(8,128)(2,1)S(1)}, u32[]{:S(2)}, u32[]{:S(2)}) async-start(bf16[16,32,128]{2,1,0:T(8,128)(2,1)} %pick.1), calls=%async_computation | async-start | bytes 262144 | tf_op jit(solution)/shard_map/all_to_all | solution.py:32
  16.0 0.0 copy-start
  16.0 1.6 %copy-done = f32[8,16,32,32]{3,2,1,0:T(8,128)S(1)} copy-done((f32[8,16,32,32]{3,2,1,0:T(8,128)S(1)}, f32[8,16,32,32]{3,2,1,0:T(8,128)}, u32[]{:S(2)}) %copy-start) | copy-done | bytes 524312
  17.6 0.0 copy-start.7
  17.6 0.0 copy-start.8
  17.6 0.0 copy-start.9
  17.6 0.0 copy-start.10
  17.7 0.0 copy-start.12
  17.7 0.7 pack_state.1
  18.4 6.3 %all-to-all-done.arrived_ref = bf16[16,32,128]{2,1,0:T(8,128)(2,1)S(1)} async-done(((bf16[16,32,128]{2,1,0:T(8,128)(2,1)}), bf16[16,32,128]{2,1,0:T(8,128)(2,1)S(1)}, u32[]{:S(2)}, u32[]{:S(2)}) %all-to-all-start) | async-done | bytes 131104 | tf_op jit(solution)/shard_map/all_to_all | solution.py:32
  24.6 0.1 add_tokens.1
  24.7 27.7 %all_to_all.20.arrived_ref.packed_ref = bf16[32,64,128]{2,1,0:T(8,128)(2,1)S(1)} all-to-all(bf16[32,64,128]{2,1,0:T(8,128)(2,1)S(1)} %add_tokens.1), channel_id=1, replica_groups=mesh['dp'=16,'row'=8,'col'=4] {'row','col'}, dimensions={0} | all-to-all | bytes 1048576 | tf_op jit(solution)/shard_map/all_to_all | solution.py:32
  52.4 0.0 copy-done.2
  52.4 0.0 copy-done.4
  52.4 0.0 copy-done.5
  52.4 0.0 copy-done.6
  52.4 0.0 copy-done.7
  52.4 0.0 copy-done.8
  52.4 0.0 copy-done.9
  52.4 0.0 copy-done.10
  52.4 0.0 copy-done.12
  52.4 1.9 %project.1 = f32[32,40,128]{2,1,0:T(8,128)S(1)} custom-call(s32[32]{0:T(128)S(1)} %copy-done.12, bf16[32,64,128]{2,1,0:T(8,128)(2,1)S(1)} %all_to_all.20.arrived_ref.packed_ref, bf16[512,576]{1,0:T(8,128)(2,1)S(1)} %bitcast.19, bf16[512,576]{1,0:T(8,128)(2,1)S(1)} %bitcast.20, bf16[1024,288]{1,0:T(8,128)(2,1)S(1)} %bitcast.17, ...), custom_call_target="tpu_custom_call" | custom-call | tf_op jit(solution)/shard_map/project/pallas_call | solution.py:378
  54.3 0.0 copy-start.1
  54.4 24.7 %all_to_all.21.arrived_ref = f32[32,40,128]{2,1,0:T(8,128)S(1)} all-to-all(f32[32,40,128]{2,1,0:T(8,128)S(1)} %project.1), channel_id=1, replica_groups=mesh['dp'=16,'row'=8,'col'=4] {'row','col'}, dimensions={0} | all-to-all | bytes 1310720 | tf_op jit(solution)/shard_map/all_to_all | solution.py:32
  79.1 1.8 %steps.1 = f32[32,24,128]{2,1,0:T(8,128)S(1)} custom-call(f32[32,40,128]{2,1,0:T(8,128)S(1)} %all_to_all.21.arrived_ref, bf16[32,64,128]{2,1,0:T(8,128)(2,1)S(1)} %all_to_all.20.arrived_ref.packed_ref), custom_call_target="tpu_custom_call" | custom-call | tf_op jit(solution)/shard_map/steps/pallas_call | solution.py:401
  80.8 18.9 %all_to_all.22 = f32[32,24,128]{2,1,0:T(8,128)S(1)} all-to-all(f32[32,24,128]{2,1,0:T(8,128)S(1)} %steps.1), channel_id=1, replica_groups=mesh['dp'=16,'row'=8,'col'=4] {'row','col'}, dimensions={0} | all-to-all | bytes 786432 | tf_op jit(solution)/shard_map/all_to_all | solution.py:32
  99.8 0.0 copy-done.1
  99.8 3.5 %finish.1 = (bf16[8,4,32,32]{3,2,1,0:T(8,128)(2,1)}, f32[8,16,32,32]{3,2,1,0:T(8,128)}) custom-call(s32[32]{0:T(128)S(1)} %copy-done.12, f32[768,128]{1,0:T(8,128)S(1)} %bitcast.16, f32[8,16,32,32]{3,2,1,0:T(8,128)S(1)} %copy-done.1), custom_call_target="tpu_custom_call" | custom-call | tf_op jit(solution)/shard_map/finish/pallas_call | solution.py:418
  (5 shorter events, 0.0 us)
Async XLA Ops:
  0.6 1.1 %copy-start.3 = (bf16[5120,72]{0,1:T(8,128)(2,1)S(1)}, bf16[5120,72]{0,1:T(8,128)(2,1)}, u32[]{:S(2)}) copy-start(bf16[5120,72]{0,1:T(8,128)(2,1)} %param.14) | copy-start | bytes 2211844
  1.7 0.7 copy-start.11
  5.6 19.1 %all-to-all-start = ((bf16[16,32,128]{2,1,0:T(8,128)(2,1)}), bf16[16,32,128]{2,1,0:T(8,128)(2,1)S(1)}, u32[]{:S(2)}, u32[]{:S(2)}) async-start(bf16[16,32,128]{2,1,0:T(8,128)(2,1)} %pick.1), calls=%async_computation | async-start | bytes 262144 | tf_op jit(solution)/shard_map/all_to_all | solution.py:32
  16.0 1.6 %copy-start = (f32[8,16,32,32]{3,2,1,0:T(8,128)S(1)}, f32[8,16,32,32]{3,2,1,0:T(8,128)}, u32[]{:S(2)}) copy-start(f32[8,16,32,32]{3,2,1,0:T(8,128)} %state_ref.3) | copy-start | bytes 1572868
  17.6 34.8 %copy-start.2 = (bf16[288,32,32]{0,2,1:T(8,128)(2,1)S(1)}, bf16[288,32,32]{0,2,1:T(8,128)(2,1)}, u32[]{:S(2)}) copy-start(bf16[288,32,32]{0,2,1:T(8,128)(2,1)} %param.17) | copy-start | bytes 1769476
  17.6 34.8 %copy-start.4 = (bf16[576,16,32]{0,2,1:T(8,128)(2,1)S(1)}, bf16[576,16,32]{0,2,1:T(8,128)(2,1)}, u32[]{:S(2)}) copy-start(bf16[576,16,32]{0,2,1:T(8,128)(2,1)} %param.15) | copy-start | bytes 1769476
  17.6 34.8 %copy-start.5 = (bf16[576,16,32]{0,2,1:T(8,128)(2,1)S(1)}, bf16[576,16,32]{0,2,1:T(8,128)(2,1)}, u32[]{:S(2)}) copy-start(bf16[576,16,32]{0,2,1:T(8,128)(2,1)} %param.16) | copy-start | bytes 1769476
  17.6 34.8 %copy-start.6 = (bf16[576,128]{1,0:T(8,128)(2,1)S(1)}, bf16[576,128]{1,0:T(8,128)(2,1)}, u32[]{:S(2)}) copy-start(bf16[576,128]{1,0:T(8,128)(2,1)} %down_ref.1) | copy-start | bytes 442372
  17.6 34.8 %copy-start.7 = (bf16[128,16,32]{0,2,1:T(8,128)(2,1)S(1)}, bf16[128,16,32]{0,2,1:T(8,128)(2,1)}, u32[]{:S(2)}) copy-start(bf16[128,16,32]{0,2,1:T(8,128)(2,1)} %param.19) | copy-start | bytes 393220
  17.6 34.8 %copy-start.8 = (bf16[576,32]{0,1:T(8,128)(2,1)S(1)}, bf16[576,32]{0,1:T(8,128)(2,1)}, u32[]{:S(2)}) copy-start(bf16[576,32]{0,1:T(8,128)(2,1)} %param.22) | copy-start | bytes 110596
  17.6 34.8 %copy-start.9 = (f32[16,32]{1,0:T(8,128)S(1)}, f32[16,32]{1,0:T(8,128)}, u32[]{:S(2)}) copy-start(f32[16,32]{1,0:T(8,128)} %bias_ref.1) | copy-start | bytes 6148
  17.6 34.8 %copy-start.10 = (f32[16,32]{1,0:T(8,128)S(1)}, f32[16,32]{1,0:T(8,128)}, u32[]{:S(2)}) copy-start(f32[16,32]{1,0:T(8,128)} %rate_ref.1) | copy-start | bytes 6148
  17.7 34.8 %copy-start.12 = (s32[32]{0:T(128)S(1)}, s32[32]{0:T(128)}, u32[]{:S(2)}) copy-start(s32[32]{0:T(128)} %heads_ref.3) | copy-start | bytes 388
  54.3 45.4 %copy-start.1 = (f32[8,16,32,32]{3,2,1,0:T(8,128)S(1)}, f32[8,16,32,32]{3,2,1,0:T(8,128)}, u32[]{:S(2)}) copy-start(f32[8,16,32,32]{3,2,1,0:T(8,128)} %state_ref.3) | copy-start | bytes 1572868

commit v4 on v3

--- a/solution.py
+++ b/solution.py
@@ -28,21 +28,34 @@
     return lax.broadcasted_iota(jnp.int32, shape, len(shape) - 2)
 
 
-def exchange(array, axis, shape=None):
+def exchange(array, axis):
     array = lax.all_to_all(array, axis, split_axis=0, concat_axis=0, tiled=True)
-    if shape is not None:
-        array = array.reshape(shape)
     return kept(array)
+
+
+def far(array):
+    return array if INTERPRET else pltpu.with_memory_space_constraint(array, pltpu.HBM)
 
 
 def kept(array):
     return array if INTERPRET else pltpu.with_memory_space_constraint(array, pltpu.VMEM)
 
 
-def pick_kernel(ids_ref, table_ref, out_ref, onehot_ref):
+def pick_kernel(ids_hbm, table_hbm, out_ref, onehot_ref, ids_ref, table_ref, sems):
     steps, streams = ids_ref.shape
     feats, vocab = table_ref.shape
     groups = out_ref.shape[0]
+    width = onehot_ref.shape[1]
+    ids_copy = pltpu.make_async_copy(ids_hbm, ids_ref, sems.at[0])
+    ids_copy.start()
+    table_copies = []
+    for part in range(vocab // width):
+        piece = pl.ds(part * width, width)
+        table_copies.append(
+            pltpu.make_async_copy(table_hbm.at[:, piece], table_ref.at[:, piece], sems.at[part + 1])
+        )
+        table_copies[-1].start()
+    ids_copy.wait()
     start = lax.axis_index("dp") * vocab
     local = jnp.broadcast_to((ids_ref[...] - start)[:, None, :], (steps, 8, streams))
     block_of = (local >> 7).astype(F32)
@@ -55,12 +68,12 @@
     blocks = jnp.concatenate(blocks, axis=0).astype(BF16)
     hits = jnp.concatenate([jnp.where(lane == place, 1.0, 0.0) for place in places], axis=0).astype(BF16)
     none = jnp.zeros_like(hits)
-    width = onehot_ref.shape[1]
     total = None
     for part in range(vocab // width):
         for k in range(width // 128):
             number = jnp.asarray(part * (width // 128) + k, BF16)
             onehot_ref[:, k * 128 : (k + 1) * 128] = jnp.where(blocks == number, hits, none)
+        table_copies[part].wait()
         found = lax.dot_general(
             onehot_ref[...], table_ref[:, part * width : (part + 1) * width], NT, preferred_element_type=F32
         )
@@ -75,28 +88,68 @@
             out_ref[:, (t - 1) * 8 : (t + 1) * 8, :] = pair.astype(BF16)
 
 
-def pack_state_kernel(state_ref, early_ref, late_ref, turned_ref):
+LEVELS = 10
+BASE = 2 * LEVELS + 1
+
+
+def rounded(array):
+    return array.astype(BF16).astype(F32)
+
+
+def left_over(array, upper):
+    share = jnp.where(upper == 0.0, 0.0, (array - upper) / jnp.where(upper == 0.0, 1.0, upper))
+    return jnp.floor(share * (256.0 * LEVELS) + 0.5)
+
+
+def joined(pair, both):
+    first = jnp.floor(both * (1.0 / BASE) + 0.5)
+    second = both - first * BASE
+    unit = 1.0 / (256.0 * LEVELS)
+    return pair[0:8] * (1.0 + first * unit), pair[8:16] * (1.0 + second * unit)
+
+
+def pack_state_kernel(state_ref, early_ref, early_rest_ref, late_ref, late_rest_ref, turned_ref):
     heads = state_ref.shape[3]
     for hi in range(2):
         for i in range(16):
             block = state_ref[hi * 4 : hi * 4 + 4, i].reshape(128, heads)
             turned_ref[pl.ds(hi * 16 + i, heads, stride=32), :] = block.T
     whole = turned_ref[...].reshape(heads, 32, 128)
-    first = whole[:, 0:16]
-    upper = first.astype(BF16)
-    early_ref[:, 0:16, :] = upper
-    early_ref[:, 16:32, :] = (first - upper.astype(F32)).astype(BF16)
-    late_ref[...] = whole[:, 16:32]
-
-
-def add_tokens_kernel(arrived_ref, early_ref, out_ref):
-    total = arrived_ref[0].astype(F32)
+    for hi, (pair_ref, rest_ref) in enumerate(((early_ref, early_rest_ref), (late_ref, late_rest_ref))):
+        half = whole[:, hi * 16 : hi * 16 + 16]
+        pair_ref[...] = half.astype(BF16)
+        left = left_over(half, rounded(half))
+        rest_ref[...] = left[:, 0:8] * BASE + left[:, 8:16]
+
+
+def add_tokens_kernel(arrived_ref, early_ref, early_rest_ref, out_ref):
+    own = arrived_ref[0].astype(F32)
     for k in range(1, arrived_ref.shape[0]):
-        total = total + arrived_ref[k].astype(F32)
-    own = total.astype(BF16)
-    out_ref[:, 0:32, :] = early_ref[...]
+        own = own + arrived_ref[k].astype(F32)
+    lane16 = lanes((16, 128))
+    lane8 = lanes((8, 128))
+    main = jnp.where(lane16 < 64, own[0:16], pltpu.roll(own[16:32], 64, 1)).astype(BF16)
+    tail = jnp.zeros((8, 128), F32)
+    for k in range(4):
+        moved = pltpu.roll(own[8 * k : 8 * k + 8], 64 + 8 * k, 1)
+        tail = jnp.where((lane8 >= 8 * k) & (lane8 < 8 * k + 8), moved, tail)
+    out_ref[:, 0:16, :] = early_ref[...]
     for p in range(out_ref.shape[0]):
-        out_ref[p, 32:64, :] = own
+        out_ref[p, 16:32, :] = jnp.concatenate([early_rest_ref[p], tail], axis=0).astype(BF16)
+        out_ref[p, 32:48, :] = main
+
+
+def token_block(arrived_ref, peer):
+    main = arrived_ref[peer, 32:48, :].astype(F32)
+    tail = arrived_ref[peer, 16:32, :].astype(F32)[8:16]
+    lane8 = lanes((8, 128))
+    turned = pltpu.roll(main, 64, 1)
+    groups = []
+    for k in range(4):
+        base = main[8 * k : 8 * k + 8] if k < 2 else turned[8 * k - 16 : 8 * k - 8]
+        moved = pltpu.roll(tail, 64 - 8 * k, 1)
+        groups.append(jnp.where(lane8 < 64, base, jnp.where(lane8 < 72, moved, 0.0)))
+    return jnp.concatenate(groups, axis=0)
 
 
 def side_by_side(blocks, width):
@@ -115,14 +168,14 @@
 
 def project_kernel(
     heads_ref, arrived_ref, query_ref, key_ref, value_ref, down_ref, up_ref, bias_ref, rate_ref, beta_ref,
-    late_ref, out_ref, mixed_ref,
+    late_ref, late_rest_ref, out_ref, mixed_ref,
 ):
     col = lax.axis_index("col")
     row = lax.axis_index("row")
     width = query_ref.shape[1] // 8
 
     def features(first, count):
-        blocks = [arrived_ref[first + k, 32:64, :].astype(F32) for k in range(count)]
+        blocks = [token_block(arrived_ref, first + k) for k in range(count)]
         return side_by_side(blocks, width)[:, : count * width].astype(BF16)
 
     own = features(col * 8, 8)
@@ -165,8 +218,12 @@
         jnp.where(wide < 64, value[256:512], jnp.where(wide < 96, value[512:768], value[768:1024])),
     )
     for slot in range(32):
-        out_ref[slot, 0:24, :] = mixed_ref[pl.ds(heads_ref[slot], 24, stride=32), :]
-    out_ref[:, 24:40, :] = late_ref[...]
+        sums = mixed_ref[pl.ds(heads_ref[slot], 24, stride=32), :]
+        upper = sums[0:16].astype(BF16)
+        out_ref[slot, 0:16, :] = upper
+        out_ref[slot, 16:32, :] = (sums[0:16] - upper.astype(F32)).astype(BF16)
+        out_ref[slot, 48:64, :] = jnp.concatenate([late_rest_ref[slot], sums[16:24]], axis=0).astype(BF16)
+    out_ref[:, 32:48, :] = late_ref[...]
 
 
 def spread(array, base):
@@ -181,9 +238,10 @@
     lane1 = lanes((1, 128))
     mixed = []
     for r in range(8):
-        total = arrived_ref[4 * r, 0:16, :]
-        for c in range(1, 4):
-            total = total + arrived_ref[4 * r + c, 0:16, :]
+        total = None
+        for c in range(4):
+            part = arrived_ref[4 * r + c, 0:16, :].astype(F32) + arrived_ref[4 * r + c, 16:32, :].astype(F32)
+            total = part if total is None else total + part
         mixed.append(total)
     mixed = jnp.concatenate(mixed, axis=0)
     below = pltpu.roll(mixed, 127, 0)
@@ -206,9 +264,17 @@
 
     values = []
     for c in range(4):
-        total = arrived_ref[c, 16:24, :]
-        for r in range(1, 8):
-            total = total + arrived_ref[4 * r + c, 16:24, :]
+        total = None
+        for r in range(8):
+            at = slice(r * 16, r * 16 + 16)
+            peer = 4 * r + c
+            rest = packed_ref[peer, 16:32, :].astype(F32)[0:8]
+            first, second = joined(packed_ref[peer, 0:16, :].astype(F32), rest)
+            state_ref[c, at, :] = jnp.concatenate([first, second], axis=0)
+            rest = arrived_ref[peer, 48:64, :].astype(F32)
+            first, second = joined(arrived_ref[peer, 32:48, :].astype(F32), rest[0:8])
+            state_ref[4 + c, at, :] = jnp.concatenate([first, second], axis=0)
+            total = rest[8:16] if total is None else total + rest[8:16]
         values.append(total)
     turned_ref[:, 0:32] = jnp.concatenate(values, axis=0).T
     turned_ref[:, 32:128] = jnp.zeros((128, 96), F32)
@@ -220,13 +286,6 @@
             for c in range(4):
                 moved = pltpu.roll(part, (target - c * 8) % 128, 1)
                 value_rows[c] = jnp.where((lane8 >= target) & (lane8 < target + 8), moved, value_rows[c])
-
-    for c in range(4):
-        for r in range(8):
-            at = slice(r * 16, r * 16 + 16)
-            upper = packed_ref[4 * r + c, 0:16, :].astype(F32)
-            state_ref[c, at, :] = upper + packed_ref[4 * r + c, 16:32, :].astype(F32)
-            state_ref[4 + c, at, :] = arrived_ref[4 * r + c, 24:40, :]
 
     for hi in range(2):
         factor = None
@@ -281,14 +340,26 @@
         upper = combined[16 * r : 16 * r + 8]
         lower = pltpu.roll(combined[16 * r + 8 : 16 * r + 16], 16, 1)
         both = jnp.where(lane8 % 32 < 16, upper, lower)
+        both_upper = rounded(both)
         for c in range(4):
-            out_ref[4 * r + c, 0:8, :] = update_ref[c]
-            out_ref[4 * r + c, 8:16, :] = result_ref[c]
-            out_ref[4 * r + c, 16:24, :] = both
-
-
-def finish_kernel(heads_ref, arrived_ref, state_ref, readout_ref, final_ref, update_ref, gain_ref, last_ref, sems):
+            update = update_ref[c]
+            update_upper = rounded(update)
+            peer = 4 * r + c
+            out_ref[peer, 0:16, :] = jnp.concatenate([update_upper, update - update_upper], axis=0).astype(BF16)
+            out_ref[peer, 16:32, :] = jnp.concatenate([both_upper, both - both_upper], axis=0).astype(BF16)
+            out_ref[peer, 32:40, :] = result_ref[c].astype(BF16)
+
+
+def finish_kernel(
+    heads_ref, packed_ref, state_ref, readout_ref, final_ref, arrived_ref, update_ref, gain_ref, last_ref, sems
+):
     heads = state_ref.shape[3]
+    for s in range(heads):
+        update = packed_ref[s, 0:16, :].astype(F32)
+        gain = packed_ref[s, 16:32, :].astype(F32)
+        arrived_ref[s * 24 : s * 24 + 8, :] = update[0:8] + update[8:16]
+        arrived_ref[s * 24 + 8 : s * 24 + 16, :] = packed_ref[s, 32:40, :].astype(F32)
+        arrived_ref[s * 24 + 16 : s * 24 + 24, :] = gain[0:8] + gain[8:16]
     for at in range(8):
         update_ref[at] = arrived_ref[pl.ds(at, heads, stride=24), :].T
         gain_ref[at] = arrived_ref[pl.ds(16 + at, heads, stride=24), :].T
@@ -347,19 +418,29 @@
     picked = pl.pallas_call(
         pick_kernel,
         out_shape=on_chip((groups, 32, 128), BF16),
-        in_specs=[VMEM, VMEM],
+        in_specs=[ANY, ANY],
         out_specs=VMEM,
-        scratch_shapes=[pltpu.VMEM((4 * token_ids.shape[0], 1024), BF16)],
+        scratch_shapes=[
+            pltpu.VMEM((4 * token_ids.shape[0], 1024), BF16),
+            pltpu.VMEM(ids.shape, jnp.int32),
+            pltpu.VMEM(table.shape, BF16),
+            pltpu.SemaphoreType.DMA((1 + table.shape[1] // 1024,)),
+        ],
         interpret=INTERPRET,
         compiler_params=pltpu.CompilerParams(vmem_limit_bytes=16 << 20),
         name="pick",
-    )(ids, table)
+    )(far(ids), far(table))
     arrived = exchange(picked, "dp")
-    early, late = pl.pallas_call(
+    early, early_rest, late, late_rest = pl.pallas_call(
         pack_state_kernel,
-        out_shape=(on_chip((32, 32, 128), BF16), on_chip((32, 16, 128), F32)),
+        out_shape=(
+            on_chip((32, 16, 128), BF16),
+            on_chip((32, 8, 128), F32),
+            on_chip((32, 16, 128), BF16),
+            on_chip((32, 8, 128), F32),
+        ),
         in_specs=[VMEM],
-        out_specs=(VMEM, VMEM),
+        out_specs=(VMEM, VMEM, VMEM, VMEM),
         scratch_shapes=[pltpu.VMEM((1024, 128), F32)],
         interpret=INTERPRET,
         compiler_params=pltpu.CompilerParams(vmem_limit_bytes=16 << 20),
@@ -367,18 +448,18 @@
     )(state)
     packed = pl.pallas_call(
         add_tokens_kernel,
-        out_shape=on_chip((32, 64, 128), BF16),
-        in_specs=[VMEM, VMEM],
+        out_shape=on_chip((32, 48, 128), BF16),
+        in_specs=[VMEM, VMEM, VMEM],
         out_specs=VMEM,
         interpret=INTERPRET,
         compiler_params=pltpu.CompilerParams(vmem_limit_bytes=16 << 20),
         name="add_tokens",
-    )(arrived, kept(early))
+    )(arrived, kept(early), kept(early_rest))
     packed = exchange(packed, BOTH)
     projected = pl.pallas_call(
         project_kernel,
-        out_shape=on_chip((32, 40, 128), F32),
-        in_specs=[SMEM] + [VMEM] * 10,
+        out_shape=on_chip((32, 64, 128), BF16),
+        in_specs=[SMEM] + [VMEM] * 11,
         out_specs=VMEM,
         scratch_shapes=[pltpu.VMEM((768, 128), F32)],
         interpret=INTERPRET,
@@ -396,11 +477,12 @@
         decay_rate,
         beta_weight.T,
         kept(late),
+        kept(late_rest),
     )
     projected = exchange(projected, BOTH)
     stepped = pl.pallas_call(
         steps_kernel,
-        out_shape=on_chip((32, 24, 128), F32),
+        out_shape=on_chip((32, 40, 128), BF16),
         in_specs=[VMEM, VMEM],
         out_specs=VMEM,
         scratch_shapes=[
@@ -414,13 +496,14 @@
         compiler_params=pltpu.CompilerParams(vmem_limit_bytes=16 << 20),
         name="steps",
     )(projected, packed)
-    stepped = exchange(stepped, BOTH, (768, 128))
+    stepped = exchange(stepped, BOTH)
     readout, final_state = pl.pallas_call(
         finish_kernel,
         out_shape=(shape_of((8, 4, 32, 32), BF16), shape_of(init_state.shape, F32)),
         in_specs=[SMEM, VMEM, VMEM],
         out_specs=(VMEM, ANY),
         scratch_shapes=[
+            pltpu.VMEM((768, 128), F32),
             pltpu.VMEM((8, 128, 32), F32),
             pltpu.VMEM((8, 128, 32), F32),
             pltpu.VMEM((8, 16, 32, 32), F32),

time: 104 us -> 97.2 us (0.935)
  blocking collectives: 71.3 us -> 64.5 us
  Pallas kernels: 11 us -> 13.2 us
  local copies, waits for them, and re-layouts: 3.43 us -> 1.64 us
    all_to_all x3, blocking collectives: 71.3 us -> 64.5 us  [exchange(): array = lax.all_to_all(array, axis, split_axis=0, concat_axis=0, tiled=True)]
    pallas_call x1, Pallas kernels: 3.14 us -> 4.96 us  [shards(): pl.pallas_call(pick_kernel, out_shape=on_chip((groups, 32, 128), BF16), i...]
    unnamed x26 -> x22, local copies, waits for them, and re-layouts: 3.43 us -> 1.64 us
where the time goes in v4:
time: 97.2 us; the launch traced here: 96.9 us
  blocking collectives  64.5 us (66%)
  Pallas kernels  13.2 us (14%)
  starting transfers between devices  10.6 us (11%)
  waiting for transfers between devices  6.21 us (6%)
  local copies, waits for them, and re-layouts  1.64 us (2%)
    all_to_all x3, blocking collectives, exchange(): array = lax.all_to_all(array, axis, split_axis=0, concat_axis=0, tiled=True)  64.5 us
    all_to_all x1, starting transfers between devices, exchange(): array = lax.all_to_all(array, axis, split_axis=0, concat_axis=0, tiled=True)  10.6 us
    all_to_all x1, waiting for transfers between devices, exchange(): array = lax.all_to_all(array, axis, split_axis=0, concat_axis=0, tiled=True)  6.21 us
    pallas_call x1, Pallas kernels, shards(): pl.pallas_call(pick_kernel, out_shape=on_chip((groups, 32, 128), BF16), i...  4.96 us
    pallas_call x1, Pallas kernels, shards(): pl.pallas_call(finish_kernel, out_shape=(shape_of((8, 4, 32, 32), BF16),...  3.51 us
    pallas_call x1, Pallas kernels, shards(): pl.pallas_call(project_kernel, out_shape=on_chip((32, 64, 128), BF16), in...  2 us
  transfers between devices with their start and end apart: 1, of which 1 were waited for; matrix products, arithmetic and copies ran while one was open for 0% of the time, Pallas kernels for 1%

profile of v4, /device:TPU:8, one launch (start us, length us, event | category | flops | bytes accessed | tf_op | source)
XLA Modules:
  0.0 96.9 jit_solution(1347696173983161254)
XLA Ops:
  0.6 5.0 %pick.1 = bf16[16,32,128]{2,1,0:T(8,128)(2,1)} custom-call(s32[4,128]{1,0:T(4,128)} %bitcast.21, bf16[72,5120]{1,0:T(8,128)(2,1)} %bitcast.20), custom_call_target="tpu_custom_call" | custom-call | tf_op jit(solution)/shard_map/pick/pallas_call | solution.py:418
  5.6 0.0 copy-start.5
  5.6 0.0 copy-start.7
  5.6 0.0 copy-start.8
  5.6 0.0 copy-start.9
  5.6 0.0 copy-start.10
  5.7 10.6 %all-to-all-start = ((bf16[16,32,128]{2,1,0:T(8,128)(2,1)}), bf16[16,32,128]{2,1,0:T(8,128)(2,1)S(1)}, u32[]{:S(2)}, u32[]{:S(2)}) async-start(bf16[16,32,128]{2,1,0:T(8,128)(2,1)} %pick.1), calls=%async_computation | async-start | bytes 262144 | tf_op jit(solution)/shard_map/all_to_all | solution.py:32
  16.2 0.0 copy-start
  16.2 1.6 %copy-done = f32[8,16,32,32]{3,2,1,0:T(8,128)S(1)} copy-done((f32[8,16,32,32]{3,2,1,0:T(8,128)S(1)}, f32[8,16,32,32]{3,2,1,0:T(8,128)}, u32[]{:S(2)}) %copy-start) | copy-done | bytes 524312
  17.8 0.0 copy-start.2
  17.8 0.0 copy-start.3
  17.8 0.0 copy-start.4
  17.8 0.8 pack_state.1
  18.7 6.2 %all-to-all-done.arrived_ref = bf16[16,32,128]{2,1,0:T(8,128)(2,1)S(1)} async-done(((bf16[16,32,128]{2,1,0:T(8,128)(2,1)}), bf16[16,32,128]{2,1,0:T(8,128)(2,1)S(1)}, u32[]{:S(2)}, u32[]{:S(2)}) %all-to-all-start) | async-done | bytes 131104 | tf_op jit(solution)/shard_map/all_to_all | solution.py:32
  24.9 0.1 add_tokens.1
  25.0 25.4 %all_to_all.20.arrived_ref.packed_ref = bf16[32,48,128]{2,1,0:T(8,128)(2,1)S(1)} all-to-all(bf16[32,48,128]{2,1,0:T(8,128)(2,1)S(1)} %add_tokens.1), channel_id=1, replica_groups=mesh['dp'=16,'row'=8,'col'=4] {'row','col'}, dimensions={0} | all-to-all | bytes 786432 | tf_op jit(solution)/shard_map/all_to_all | solution.py:32
  50.4 0.0 copy-done.5
  50.4 0.0 copy-done.7
  50.4 0.0 copy-done.8
  50.4 0.0 copy-done.9
  50.4 0.0 copy-done.10
  50.4 0.0 copy-done.2
  50.4 0.0 copy-done.3
  50.4 0.0 copy-done.4
  50.4 0.0 copy-done.6
  50.4 2.0 %project.1 = bf16[32,64,128]{2,1,0:T(8,128)(2,1)S(1)} custom-call(s32[32]{0:T(128)S(1)} %copy-done.10, bf16[32,48,128]{2,1,0:T(8,128)(2,1)S(1)} %all_to_all.20.arrived_ref.packed_ref, bf16[512,576]{1,0:T(8,128)(2,1)S(1)} %bitcast.16, bf16[512,576]{1,0:T(8,128)(2,1)S(1)} %bitcast.17, bf16[1024,288]{1,0:T(8,128)(2,1)S(1)} %bitcast.15, ...), custom_call_target="tpu_custom_call" | custom-call | tf_op jit(solution)/shard_map/project/pallas_call | solution.py:459
  52.4 0.0 copy-start.1
  52.4 21.6 %all_to_all.21.arrived_ref = bf16[32,64,128]{2,1,0:T(8,128)(2,1)S(1)} all-to-all(bf16[32,64,128]{2,1,0:T(8,128)(2,1)S(1)} %project.1), channel_id=1, replica_groups=mesh['dp'=16,'row'=8,'col'=4] {'row','col'}, dimensions={0} | all-to-all | bytes 1048576 | tf_op jit(solution)/shard_map/all_to_all | solution.py:32
  74.0 1.8 %steps.1 = bf16[32,40,128]{2,1,0:T(8,128)(2,1)S(1)} custom-call(bf16[32,64,128]{2,1,0:T(8,128)(2,1)S(1)} %all_to_all.21.arrived_ref, bf16[32,48,128]{2,1,0:T(8,128)(2,1)S(1)} %all_to_all.20.arrived_ref.packed_ref), custom_call_target="tpu_custom_call" | custom-call | tf_op jit(solution)/shard_map/steps/pallas_call | solution.py:483
  75.8 17.5 %all_to_all.22.packed_ref = bf16[32,40,128]{2,1,0:T(8,128)(2,1)S(1)} all-to-all(bf16[32,40,128]{2,1,0:T(8,128)(2,1)S(1)} %steps.1), channel_id=1, replica_groups=mesh['dp'=16,'row'=8,'col'=4] {'row','col'}, dimensions={0} | all-to-all | bytes 655360 | tf_op jit(solution)/shard_map/all_to_all | solution.py:32
  93.3 0.0 copy-done.1
  93.3 3.5 %finish.1 = (bf16[8,4,32,32]{3,2,1,0:T(8,128)(2,1)}, f32[8,16,32,32]{3,2,1,0:T(8,128)}) custom-call(s32[32]{0:T(128)S(1)} %copy-done.10, bf16[32,40,128]{2,1,0:T(8,128)(2,1)S(1)} %all_to_all.22.packed_ref, f32[8,16,32,32]{3,2,1,0:T(8,128)S(1)} %copy-done.1), custom_call_target="tpu_custom_call" | custom-call | tf_op jit(solution)/shard_map/finish/pallas_call | solution.py:500
  (1 shorter events, 0.0 us)
Async XLA Ops:
  5.6 44.8 %copy-start.5 = (bf16[576,128]{1,0:T(8,128)(2,1)S(1)}, bf16[576,128]{1,0:T(8,128)(2,1)}, u32[]{:S(2)}) copy-start(bf16[576,128]{1,0:T(8,128)(2,1)} %down_ref.1) | copy-start | bytes 442372
  5.6 44.7 %copy-start.7 = (bf16[576,32]{0,1:T(8,128)(2,1)S(1)}, bf16[576,32]{0,1:T(8,128)(2,1)}, u32[]{:S(2)}) copy-start(bf16[576,32]{0,1:T(8,128)(2,1)} %param.22) | copy-start | bytes 110596
  5.6 44.7 %copy-start.8 = (f32[16,32]{1,0:T(8,128)S(1)}, f32[16,32]{1,0:T(8,128)}, u32[]{:S(2)}) copy-start(f32[16,32]{1,0:T(8,128)} %bias_ref.1) | copy-start | bytes 6148
  5.6 44.7 %copy-start.9 = (f32[16,32]{1,0:T(8,128)S(1)}, f32[16,32]{1,0:T(8,128)}, u32[]{:S(2)}) copy-start(f32[16,32]{1,0:T(8,128)} %rate_ref.1) | copy-start | bytes 6148
  5.6 44.7 %copy-start.10 = (s32[32]{0:T(128)S(1)}, s32[32]{0:T(128)}, u32[]{:S(2)}) copy-start(s32[32]{0:T(128)} %heads_ref.3) | copy-start | bytes 388
  5.7 19.2 %all-to-all-start = ((bf16[16,32,128]{2,1,0:T(8,128)(2,1)}), bf16[16,32,128]{2,1,0:T(8,128)(2,1)S(1)}, u32[]{:S(2)}, u32[]{:S(2)}) async-start(bf16[16,32,128]{2,1,0:T(8,128)(2,1)} %pick.1), calls=%async_computation | async-start | bytes 262144 | tf_op jit(solution)/shard_map/all_to_all | solution.py:32
  16.2 1.6 %copy-start = (f32[8,16,32,32]{3,2,1,0:T(8,128)S(1)}, f32[8,16,32,32]{3,2,1,0:T(8,128)}, u32[]{:S(2)}) copy-start(f32[8,16,32,32]{3,2,1,0:T(8,128)} %state_ref.3) | copy-start | bytes 1572868
  17.8 32.6 %copy-start.2 = (bf16[288,32,32]{0,2,1:T(8,128)(2,1)S(1)}, bf16[288,32,32]{0,2,1:T(8,128)(2,1)}, u32[]{:S(2)}) copy-start(bf16[288,32,32]{0,2,1:T(8,128)(2,1)} %param.17) | copy-start | bytes 1769476
  17.8 32.6 %copy-start.3 = (bf16[576,16,32]{0,2,1:T(8,128)(2,1)S(1)}, bf16[576,16,32]{0,2,1:T(8,128)(2,1)}, u32[]{:S(2)}) copy-start(bf16[576,16,32]{0,2,1:T(8,128)(2,1)} %param.15) | copy-start | bytes 1769476
  17.8 32.6 %copy-start.4 = (bf16[576,16,32]{0,2,1:T(8,128)(2,1)S(1)}, bf16[576,16,32]{0,2,1:T(8,128)(2,1)}, u32[]{:S(2)}) copy-start(bf16[576,16,32]{0,2,1:T(8,128)(2,1)} %param.16) | copy-start | bytes 1769476
  17.8 32.6 %copy-start.6 = (bf16[128,16,32]{0,2,1:T(8,128)(2,1)S(1)}, bf16[128,16,32]{0,2,1:T(8,128)(2,1)}, u32[]{:S(2)}) copy-start(bf16[128,16,32]{0,2,1:T(8,128)(2,1)} %param.19) | copy-start | bytes 393220
  52.4 40.9 %copy-start.1 = (f32[8,16,32,32]{3,2,1,0:T(8,128)S(1)}, f32[8,16,32,32]{3,2,1,0:T(8,128)}, u32[]{:S(2)}) copy-start(f32[8,16,32,32]{3,2,1,0:T(8,128)} %state_ref.3) | copy-start | bytes 1572868

commit v5 on v4

--- a/solution.py
+++ b/solution.py
@@ -45,47 +45,29 @@
     steps, streams = ids_ref.shape
     feats, vocab = table_ref.shape
     groups = out_ref.shape[0]
-    width = onehot_ref.shape[1]
     ids_copy = pltpu.make_async_copy(ids_hbm, ids_ref, sems.at[0])
+    table_copy = pltpu.make_async_copy(table_hbm, table_ref, sems.at[1])
     ids_copy.start()
-    table_copies = []
-    for part in range(vocab // width):
-        piece = pl.ds(part * width, width)
-        table_copies.append(
-            pltpu.make_async_copy(table_hbm.at[:, piece], table_ref.at[:, piece], sems.at[part + 1])
-        )
-        table_copies[-1].start()
+    table_copy.start()
     ids_copy.wait()
     start = lax.axis_index("dp") * vocab
-    local = jnp.broadcast_to((ids_ref[...] - start)[:, None, :], (steps, 8, streams))
-    block_of = (local >> 7).astype(F32)
-    place_of = (local & 127).astype(F32)
-    blocks, places = [], []
+    wide = jnp.broadcast_to((ids_ref[...] - start).astype(F32)[:, None, :], (steps, 8, streams))
+    width = 1024
     for t in range(steps):
-        blocks.append(jnp.broadcast_to(block_of[t].T[:, 0:1], (streams, 128)))
-        places.append(place_of[t].T[:, 0:1])
-    lane = lanes((streams, 128)).astype(F32)
-    blocks = jnp.concatenate(blocks, axis=0).astype(BF16)
-    hits = jnp.concatenate([jnp.where(lane == place, 1.0, 0.0) for place in places], axis=0).astype(BF16)
-    none = jnp.zeros_like(hits)
-    total = None
-    for part in range(vocab // width):
-        for k in range(width // 128):
-            number = jnp.asarray(part * (width // 128) + k, BF16)
-            onehot_ref[:, k * 128 : (k + 1) * 128] = jnp.where(blocks == number, hits, none)
-        table_copies[part].wait()
-        found = lax.dot_general(
-            onehot_ref[...], table_ref[:, part * width : (part + 1) * width], NT, preferred_element_type=F32
-        )
-        total = found if total is None else total + found
-    wide = jnp.concatenate([total, jnp.zeros((total.shape[0], 128 - feats), F32)], axis=1)
-    for t in range(steps):
-        block = wide[t * streams : (t + 1) * streams].reshape(groups, 8, 128)
-        if t % 2 == 0:
-            held = block
-        else:
-            pair = jnp.concatenate([held, block], axis=1)
-            out_ref[:, (t - 1) * 8 : (t + 1) * 8, :] = pair.astype(BF16)
+        column = wide[t].T.astype(jnp.int32)[:, 0:1]
+        for part in range(vocab // width):
+            hit = column == lanes((streams, width)) + part * width
+            onehot_ref[t * streams : (t + 1) * streams, part * width : (part + 1) * width] = jnp.where(
+                hit, 1.0, 0.0
+            ).astype(BF16)
+    table_copy.wait()
+    total = lax.dot_general(onehot_ref[...], table_ref[...], NT, preferred_element_type=F32)
+    total = jnp.concatenate([total, jnp.zeros((total.shape[0], 128 - feats), F32)], axis=1)
+    for t in range(0, steps, 2):
+        pair = [
+            total[k * streams : (k + 1) * streams].reshape(groups, 8, 128) for k in (t, t + 1)
+        ]
+        out_ref[:, t * 8 : t * 8 + 16, :] = jnp.concatenate(pair, axis=1).astype(BF16)
 
 
 LEVELS = 10
@@ -106,6 +88,11 @@
     second = both - first * BASE
     unit = 1.0 / (256.0 * LEVELS)
     return pair[0:8] * (1.0 + first * unit), pair[8:16] * (1.0 + second * unit)
+
+
+def left_of_both(array):
+    left = left_over(array, rounded(array))
+    return left[0:8] * BASE + left[8:16]
 
 
 def pack_state_kernel(state_ref, early_ref, early_rest_ref, late_ref, late_rest_ref, turned_ref):
@@ -119,7 +106,7 @@
         half = whole[:, hi * 16 : hi * 16 + 16]
         pair_ref[...] = half.astype(BF16)
         left = left_over(half, rounded(half))
-        rest_ref[...] = left[:, 0:8] * BASE + left[:, 8:16]
+        rest_ref[...] = (left[:, 0:8] * BASE + left[:, 8:16]).astype(rest_ref.dtype)
 
 
 def add_tokens_kernel(arrived_ref, early_ref, early_rest_ref, out_ref):
@@ -219,11 +206,11 @@
     )
     for slot in range(32):
         sums = mixed_ref[pl.ds(heads_ref[slot], 24, stride=32), :]
-        upper = sums[0:16].astype(BF16)
-        out_ref[slot, 0:16, :] = upper
-        out_ref[slot, 16:32, :] = (sums[0:16] - upper.astype(F32)).astype(BF16)
-        out_ref[slot, 48:64, :] = jnp.concatenate([late_rest_ref[slot], sums[16:24]], axis=0).astype(BF16)
+        out_ref[slot, 0:16, :] = sums[0:16].astype(BF16)
+        rest = left_of_both(sums[0:16])
+        out_ref[slot, 16:32, :] = jnp.concatenate([rest, sums[16:24]], axis=0).astype(BF16)
     out_ref[:, 32:48, :] = late_ref[...]
+    out_ref[:, 48:56, :] = late_rest_ref[...]
 
 
 def spread(array, base):
@@ -240,7 +227,9 @@
     for r in range(8):
         total = None
         for c in range(4):
-            part = arrived_ref[4 * r + c, 0:16, :].astype(F32) + arrived_ref[4 * r + c, 16:32, :].astype(F32)
+            peer = 4 * r + c
+            rest = arrived_ref[peer, 16:32, :].astype(F32)[0:8]
+            part = jnp.concatenate(joined(arrived_ref[peer, 0:16, :].astype(F32), rest), axis=0)
             total = part if total is None else total + part
         mixed.append(total)
     mixed = jnp.concatenate(mixed, axis=0)
@@ -271,10 +260,11 @@
             rest = packed_ref[peer, 16:32, :].astype(F32)[0:8]
             first, second = joined(packed_ref[peer, 0:16, :].astype(F32), rest)
             state_ref[c, at, :] = jnp.concatenate([first, second], axis=0)
-            rest = arrived_ref[peer, 48:64, :].astype(F32)
-            first, second = joined(arrived_ref[peer, 32:48, :].astype(F32), rest[0:8])
+            rest = arrived_ref[peer, 48:56, :].astype(F32)
+            first, second = joined(arrived_ref[peer, 32:48, :].astype(F32), rest)
             state_ref[4 + c, at, :] = jnp.concatenate([first, second], axis=0)
-            total = rest[8:16] if total is None else total + rest[8:16]
+            part = arrived_ref[peer, 16:32, :].astype(F32)[8:16]
+            total = part if total is None else total + part
         values.append(total)
     turned_ref[:, 0:32] = jnp.concatenate(values, axis=0).T
     turned_ref[:, 32:128] = jnp.zeros((128, 96), F32)
@@ -340,34 +330,33 @@
         upper = combined[16 * r : 16 * r + 8]
         lower = pltpu.roll(combined[16 * r + 8 : 16 * r + 16], 16, 1)
         both = jnp.where(lane8 % 32 < 16, upper, lower)
-        both_upper = rounded(both)
         for c in range(4):
-            update = update_ref[c]
-            update_upper = rounded(update)
-            peer = 4 * r + c
-            out_ref[peer, 0:16, :] = jnp.concatenate([update_upper, update - update_upper], axis=0).astype(BF16)
-            out_ref[peer, 16:32, :] = jnp.concatenate([both_upper, both - both_upper], axis=0).astype(BF16)
-            out_ref[peer, 32:40, :] = result_ref[c].astype(BF16)
+            pair = jnp.concatenate([update_ref[c], both], axis=0)
+            rest = jnp.concatenate([left_of_both(pair), result_ref[c]], axis=0)
+            out_ref[4 * r + c, 0:16, :] = pair.astype(BF16)
+            out_ref[4 * r + c, 16:32, :] = rest.astype(BF16)
 
 
 def finish_kernel(
-    heads_ref, packed_ref, state_ref, readout_ref, final_ref, arrived_ref, update_ref, gain_ref, last_ref, sems
+    heads_ref, packed_ref, state_ref, readout_hbm, final_hbm,
+    arrived_ref, update_ref, gain_ref, readout_ref, final_ref, sems,
 ):
     heads = state_ref.shape[3]
     for s in range(heads):
-        update = packed_ref[s, 0:16, :].astype(F32)
-        gain = packed_ref[s, 16:32, :].astype(F32)
-        arrived_ref[s * 24 : s * 24 + 8, :] = update[0:8] + update[8:16]
-        arrived_ref[s * 24 + 8 : s * 24 + 16, :] = packed_ref[s, 32:40, :].astype(F32)
-        arrived_ref[s * 24 + 16 : s * 24 + 24, :] = gain[0:8] + gain[8:16]
+        rest = packed_ref[s, 16:32, :].astype(F32)
+        update, gain = joined(packed_ref[s, 0:16, :].astype(F32), rest[0:8])
+        arrived_ref[s * 24 : s * 24 + 8, :] = update
+        arrived_ref[s * 24 + 8 : s * 24 + 16, :] = gain
+        arrived_ref[s * 24 + 16 : s * 24 + 24, :] = rest[8:16]
     for at in range(8):
-        update_ref[at] = arrived_ref[pl.ds(at, heads, stride=24), :].T
-        gain_ref[at] = arrived_ref[pl.ds(16 + at, heads, stride=24), :].T
+        gain_ref[at] = arrived_ref[pl.ds(8 + at, heads, stride=24), :].T
     copies = []
     for hi in range(2):
+        for t in range(4):
+            update_ref[t] = arrived_ref[pl.ds(t * 2 + hi, heads, stride=24), :].T
         for lo in range(4):
             stream = hi * 4 + lo
-            updates = [update_ref[t * 2 + hi, lo * 32 : lo * 32 + 32, :] for t in range(4)]
+            updates = [update_ref[t, lo * 32 : lo * 32 + 32, :] for t in range(4)]
             for i in range(16):
                 i_hi, i_lo = divmod(i, 8)
                 base = lo * 32 + i_hi * 16
@@ -375,8 +364,8 @@
                 for t in range(4):
                     at = base + t * 2 + hi
                     total = total + gain_ref[i_lo, at : at + 1, :] * updates[t]
-                last_ref[stream, i] = total
-            copies.append(pltpu.make_async_copy(last_ref.at[stream], final_ref.at[stream], sems.at[stream]))
+                final_ref[stream, i] = total
+            copies.append(pltpu.make_async_copy(final_ref.at[stream], final_hbm.at[stream], sems.at[stream]))
             copies[-1].start()
     slot = rows_of((heads, heads))
     head = lanes((heads, heads))
@@ -386,10 +375,12 @@
     order = order.astype(BF16)
     for at in range(8):
         t, hi = divmod(at, 2)
-        result = arrived_ref[pl.ds(8 + at, heads, stride=24), :].astype(BF16)
+        result = arrived_ref[pl.ds(16 + at, heads, stride=24), :].astype(BF16)
         turned = lax.dot_general(result, order, TN, preferred_element_type=F32).astype(BF16)
         for lo in range(4):
             readout_ref[hi * 4 + lo, t] = turned[lo * 32 : lo * 32 + 32]
+    copies.append(pltpu.make_async_copy(readout_ref, readout_hbm, sems.at[8]))
+    copies[-1].start()
     for copy in copies:
         copy.wait()
 
@@ -421,10 +412,10 @@
         in_specs=[ANY, ANY],
         out_specs=VMEM,
         scratch_shapes=[
-            pltpu.VMEM((4 * token_ids.shape[0], 1024), BF16),
+            pltpu.VMEM((4 * token_ids.shape[0], table.shape[1]), BF16),
             pltpu.VMEM(ids.shape, jnp.int32),
             pltpu.VMEM(table.shape, BF16),
-            pltpu.SemaphoreType.DMA((1 + table.shape[1] // 1024,)),
+            pltpu.SemaphoreType.DMA((2,)),
         ],
         interpret=INTERPRET,
         compiler_params=pltpu.CompilerParams(vmem_limit_bytes=16 << 20),
@@ -437,7 +428,7 @@
             on_chip((32, 16, 128), BF16),
             on_chip((32, 8, 128), F32),
             on_chip((32, 16, 128), BF16),
-            on_chip((32, 8, 128), F32),
+            on_chip((32, 8, 128), BF16),
         ),
         in_specs=[VMEM],
         out_specs=(VMEM, VMEM, VMEM, VMEM),
@@ -458,7 +449,7 @@
     packed = exchange(packed, BOTH)
     projected = pl.pallas_call(
         project_kernel,
-        out_shape=on_chip((32, 64, 128), BF16),
+        out_shape=on_chip((32, 56, 128), BF16),
         in_specs=[SMEM] + [VMEM] * 11,
         out_specs=VMEM,
         scratch_shapes=[pltpu.VMEM((768, 128), F32)],
@@ -482,7 +473,7 @@
     projected = exchange(projected, BOTH)
     stepped = pl.pallas_call(
         steps_kernel,
-        out_shape=on_chip((32, 40, 128), BF16),
+        out_shape=on_chip((32, 32, 128), BF16),
         in_specs=[VMEM, VMEM],
         out_specs=VMEM,
         scratch_shapes=[
@@ -501,13 +492,14 @@
         finish_kernel,
         out_shape=(shape_of((8, 4, 32, 32), BF16), shape_of(init_state.shape, F32)),
         in_specs=[SMEM, VMEM, VMEM],
-        out_specs=(VMEM, ANY),
+        out_specs=(ANY, ANY),
         scratch_shapes=[
             pltpu.VMEM((768, 128), F32),
+            pltpu.VMEM((4, 128, 32), F32),
             pltpu.VMEM((8, 128, 32), F32),
-            pltpu.VMEM((8, 128, 32), F32),
+            pltpu.VMEM((8, 4, 32, 32), BF16),
             pltpu.VMEM((8, 16, 32, 32), F32),
-            pltpu.SemaphoreType.DMA((8,)),
+            pltpu.SemaphoreType.DMA((9,)),
         ],
         interpret=INTERPRET,
         compiler_params=pltpu.CompilerParams(vmem_limit_bytes=16 << 20),

time: 97.2 us -> 92.6 us (0.953)
  blocking collectives: 64.5 us -> 61.9 us
  Pallas kernels: 13.2 us -> 11.2 us
    all_to_all x3, blocking collectives: 64.5 us -> 61.9 us  [exchange(): array = lax.all_to_all(array, axis, split_axis=0, concat_axis=0, tiled=True)]
    pallas_call x1, Pallas kernels: 4.96 us -> 3.41 us  [shards(): pl.pallas_call(pick_kernel, out_shape=on_chip((groups, 32, 128), BF16), i...]
where the time goes in v5:
time: 92.6 us; the launch traced here: 92.2 us
  blocking collectives  61.9 us (67%)
  Pallas kernels  11.2 us (12%)
  starting transfers between devices  10.6 us (11%)
  waiting for transfers between devices  6.2 us (7%)
  local copies, waits for them, and re-layouts  1.64 us (2%)
    all_to_all x3, blocking collectives, exchange(): array = lax.all_to_all(array, axis, split_axis=0, concat_axis=0, tiled=True)  61.9 us
    all_to_all x1, starting transfers between devices, exchange(): array = lax.all_to_all(array, axis, split_axis=0, concat_axis=0, tiled=True)  10.6 us
    all_to_all x1, waiting for transfers between devices, exchange(): array = lax.all_to_all(array, axis, split_axis=0, concat_axis=0, tiled=True)  6.2 us
    pallas_call x1, Pallas kernels, shards(): pl.pallas_call(pick_kernel, out_shape=on_chip((groups, 32, 128), BF16), i...  3.41 us
    pallas_call x1, Pallas kernels, shards(): pl.pallas_call(finish_kernel, out_shape=(shape_of((8, 4, 32, 32), BF16),...  3 us
    pallas_call x1, Pallas kernels, shards(): pl.pallas_call(project_kernel, out_shape=on_chip((32, 56, 128), BF16), in...  2 us
  transfers between devices with their start and end apart: 1, of which 1 were waited for; matrix products, arithmetic and copies ran while one was open for 0% of the time, Pallas kernels for 1%

profile of v5, /device:TPU:8, one launch (start us, length us, event | category | flops | bytes accessed | tf_op | source)
XLA Modules:
  0.0 92.2 jit_solution(11788557854365209737)
XLA Ops:
  0.6 3.4 %pick.1 = bf16[16,32,128]{2,1,0:T(8,128)(2,1)} custom-call(s32[4,128]{1,0:T(4,128)} %bitcast.21, bf16[72,5120]{1,0:T(8,128)(2,1)} %bitcast.20), custom_call_target="tpu_custom_call" | custom-call | tf_op jit(solution)/shard_map/pick/pallas_call | solution.py:409
  4.0 0.0 copy-start.5
  4.1 0.0 copy-start.7
  4.1 0.0 copy-start.8
  4.1 0.0 copy-start.9
  4.1 0.0 copy-start.10
  4.1 10.6 %all-to-all-start = ((bf16[16,32,128]{2,1,0:T(8,128)(2,1)}), bf16[16,32,128]{2,1,0:T(8,128)(2,1)S(1)}, u32[]{:S(2)}, u32[]{:S(2)}) async-start(bf16[16,32,128]{2,1,0:T(8,128)(2,1)} %pick.1), calls=%async_computation | async-start | bytes 262144 | tf_op jit(solution)/shard_map/all_to_all | solution.py:32
  14.7 0.0 copy-start
  14.7 1.6 %copy-done = f32[8,16,32,32]{3,2,1,0:T(8,128)S(1)} copy-done((f32[8,16,32,32]{3,2,1,0:T(8,128)S(1)}, f32[8,16,32,32]{3,2,1,0:T(8,128)}, u32[]{:S(2)}) %copy-start) | copy-done | bytes 524312
  16.3 0.0 copy-start.2
  16.3 0.0 copy-start.3
  16.3 0.0 copy-start.4
  16.3 0.8 pack_state.1
  17.1 6.2 %all-to-all-done.arrived_ref = bf16[16,32,128]{2,1,0:T(8,128)(2,1)S(1)} async-done(((bf16[16,32,128]{2,1,0:T(8,128)(2,1)}), bf16[16,32,128]{2,1,0:T(8,128)(2,1)S(1)}, u32[]{:S(2)}, u32[]{:S(2)}) %all-to-all-start) | async-done | bytes 131104 | tf_op jit(solution)/shard_map/all_to_all | solution.py:32
  23.3 0.1 add_tokens.1
  23.4 25.4 %all_to_all.20.arrived_ref.packed_ref = bf16[32,48,128]{2,1,0:T(8,128)(2,1)S(1)} all-to-all(bf16[32,48,128]{2,1,0:T(8,128)(2,1)S(1)} %add_tokens.1), channel_id=1, replica_groups=mesh['dp'=16,'row'=8,'col'=4] {'row','col'}, dimensions={0} | all-to-all | bytes 786432 | tf_op jit(solution)/shard_map/all_to_all | solution.py:32
  48.8 0.0 copy-done.5
  48.8 0.0 copy-done.7
  48.8 0.0 copy-done.8
  48.8 0.0 copy-done.9
  48.8 0.0 copy-done.10
  48.8 0.0 copy-done.2
  48.8 0.0 copy-done.3
  48.8 0.0 copy-done.4
  48.9 0.0 copy-done.6
  48.9 2.0 %project.1 = bf16[32,56,128]{2,1,0:T(8,128)(2,1)S(1)} custom-call(s32[32]{0:T(128)S(1)} %copy-done.10, bf16[32,48,128]{2,1,0:T(8,128)(2,1)S(1)} %all_to_all.20.arrived_ref.packed_ref, bf16[512,576]{1,0:T(8,128)(2,1)S(1)} %bitcast.16, bf16[512,576]{1,0:T(8,128)(2,1)S(1)} %bitcast.17, bf16[1024,288]{1,0:T(8,128)(2,1)S(1)} %bitcast.15, ...), custom_call_target="tpu_custom_call" | custom-call | tf_op jit(solution)/shard_map/project/pallas_call | solution.py:450
  50.9 0.0 copy-start.1
  50.9 20.4 %all_to_all.21.arrived_ref = bf16[32,56,128]{2,1,0:T(8,128)(2,1)S(1)} all-to-all(bf16[32,56,128]{2,1,0:T(8,128)(2,1)S(1)} %project.1), channel_id=1, replica_groups=mesh['dp'=16,'row'=8,'col'=4] {'row','col'}, dimensions={0} | all-to-all | bytes 917504 | tf_op jit(solution)/shard_map/all_to_all | solution.py:32
  71.3 1.8 %steps.1 = bf16[32,32,128]{2,1,0:T(8,128)(2,1)S(1)} custom-call(bf16[32,56,128]{2,1,0:T(8,128)(2,1)S(1)} %all_to_all.21.arrived_ref, bf16[32,48,128]{2,1,0:T(8,128)(2,1)S(1)} %all_to_all.20.arrived_ref.packed_ref), custom_call_target="tpu_custom_call" | custom-call | tf_op jit(solution)/shard_map/steps/pallas_call | solution.py:474
  73.1 16.1 %all_to_all.22.packed_ref = bf16[32,32,128]{2,1,0:T(8,128)(2,1)S(1)} all-to-all(bf16[32,32,128]{2,1,0:T(8,128)(2,1)S(1)} %steps.1), channel_id=1, replica_groups=mesh['dp'=16,'row'=8,'col'=4] {'row','col'}, dimensions={0} | all-to-all | bytes 524288 | tf_op jit(solution)/shard_map/all_to_all | solution.py:32
  89.2 0.0 copy-done.1
  89.2 3.0 %finish.1 = (bf16[8,4,32,32]{3,2,1,0:T(8,128)(2,1)}, f32[8,16,32,32]{3,2,1,0:T(8,128)}) custom-call(s32[32]{0:T(128)S(1)} %copy-done.10, bf16[32,32,128]{2,1,0:T(8,128)(2,1)S(1)} %all_to_all.22.packed_ref, f32[8,16,32,32]{3,2,1,0:T(8,128)S(1)} %copy-done.1), custom_call_target="tpu_custom_call" | custom-call | tf_op jit(solution)/shard_map/finish/pallas_call | solution.py:491
  (1 shorter events, 0.0 us)
Async XLA Ops:
  4.0 44.8 %copy-start.5 = (bf16[576,128]{1,0:T(8,128)(2,1)S(1)}, bf16[576,128]{1,0:T(8,128)(2,1)}, u32[]{:S(2)}) copy-start(bf16[576,128]{1,0:T(8,128)(2,1)} %down_ref.1) | copy-start | bytes 442372
  4.1 44.7 %copy-start.7 = (bf16[576,32]{0,1:T(8,128)(2,1)S(1)}, bf16[576,32]{0,1:T(8,128)(2,1)}, u32[]{:S(2)}) copy-start(bf16[576,32]{0,1:T(8,128)(2,1)} %param.22) | copy-start | bytes 110596
  4.1 44.7 %copy-start.8 = (f32[16,32]{1,0:T(8,128)S(1)}, f32[16,32]{1,0:T(8,128)}, u32[]{:S(2)}) copy-start(f32[16,32]{1,0:T(8,128)} %bias_ref.1) | copy-start | bytes 6148
  4.1 44.7 %copy-start.9 = (f32[16,32]{1,0:T(8,128)S(1)}, f32[16,32]{1,0:T(8,128)}, u32[]{:S(2)}) copy-start(f32[16,32]{1,0:T(8,128)} %rate_ref.1) | copy-start | bytes 6148
  4.1 44.7 %copy-start.10 = (s32[32]{0:T(128)S(1)}, s32[32]{0:T(128)}, u32[]{:S(2)}) copy-start(s32[32]{0:T(128)} %heads_ref.3) | copy-start | bytes 388
  4.1 19.2 %all-to-all-start = ((bf16[16,32,128]{2,1,0:T(8,128)(2,1)}), bf16[16,32,128]{2,1,0:T(8,128)(2,1)S(1)}, u32[]{:S(2)}, u32[]{:S(2)}) async-start(bf16[16,32,128]{2,1,0:T(8,128)(2,1)} %pick.1), calls=%async_computation | async-start | bytes 262144 | tf_op jit(solution)/shard_map/all_to_all | solution.py:32
  14.7 1.6 %copy-start = (f32[8,16,32,32]{3,2,1,0:T(8,128)S(1)}, f32[8,16,32,32]{3,2,1,0:T(8,128)}, u32[]{:S(2)}) copy-start(f32[8,16,32,32]{3,2,1,0:T(8,128)} %state_ref.3) | copy-start | bytes 1572868
  16.3 32.6 %copy-start.2 = (bf16[288,32,32]{0,2,1:T(8,128)(2,1)S(1)}, bf16[288,32,32]{0,2,1:T(8,128)(2,1)}, u32[]{:S(2)}) copy-start(bf16[288,32,32]{0,2,1:T(8,128)(2,1)} %param.17) | copy-start | bytes 1769476
  16.3 32.6 %copy-start.3 = (bf16[576,16,32]{0,2,1:T(8,128)(2,1)S(1)}, bf16[576,16,32]{0,2,1:T(8,128)(2,1)}, u32[]{:S(2)}) copy-start(bf16[576,16,32]{0,2,1:T(8,128)(2,1)} %param.15) | copy-start | bytes 1769476
  16.3 32.6 %copy-start.4 = (bf16[576,16,32]{0,2,1:T(8,128)(2,1)S(1)}, bf16[576,16,32]{0,2,1:T(8,128)(2,1)}, u32[]{:S(2)}) copy-start(bf16[576,16,32]{0,2,1:T(8,128)(2,1)} %param.16) | copy-start | bytes 1769476
  16.3 32.6 %copy-start.6 = (bf16[128,16,32]{0,2,1:T(8,128)(2,1)S(1)}, bf16[128,16,32]{0,2,1:T(8,128)(2,1)}, u32[]{:S(2)}) copy-start(bf16[128,16,32]{0,2,1:T(8,128)(2,1)} %param.19) | copy-start | bytes 393220
  50.9 38.3 %copy-start.1 = (f32[8,16,32,32]{3,2,1,0:T(8,128)S(1)}, f32[8,16,32,32]{3,2,1,0:T(8,128)}, u32[]{:S(2)}) copy-start(f32[8,16,32,32]{3,2,1,0:T(8,128)} %state_ref.3) | copy-start | bytes 1572868

commit v6 on v5

--- a/solution.py
+++ b/solution.py
@@ -109,7 +109,7 @@
         rest_ref[...] = (left[:, 0:8] * BASE + left[:, 8:16]).astype(rest_ref.dtype)
 
 
-def add_tokens_kernel(arrived_ref, early_ref, early_rest_ref, out_ref):
+def add_tokens_kernel(arrived_ref, early_ref, early_rest_ref, late_rest_ref, out_ref):
     own = arrived_ref[0].astype(F32)
     for k in range(1, arrived_ref.shape[0]):
         own = own + arrived_ref[k].astype(F32)
@@ -122,7 +122,8 @@
         tail = jnp.where((lane8 >= 8 * k) & (lane8 < 8 * k + 8), moved, tail)
     out_ref[:, 0:16, :] = early_ref[...]
     for p in range(out_ref.shape[0]):
-        out_ref[p, 16:32, :] = jnp.concatenate([early_rest_ref[p], tail], axis=0).astype(BF16)
+        spare = jnp.where(lane8 < 32, tail, late_rest_ref[p])
+        out_ref[p, 16:32, :] = jnp.concatenate([early_rest_ref[p], spare], axis=0).astype(BF16)
         out_ref[p, 32:48, :] = main
 
 
@@ -188,10 +189,12 @@
     for ch in range(16):
         at = slice(ch * 32, ch * 32 + 32)
         misc = beta
-        if ch > 0:
-            misc = jnp.broadcast_to(rate[:, ch : ch + 1], (32, 128))
+        if 0 < ch < 8:
+            misc = jnp.where(lane == 96, rate[:, ch : ch + 1], rate[:, ch + 8 : ch + 9])
         if ch == 1:
-            misc = jnp.where(lane == 97, rate[:, 0:1], misc)
+            misc = jnp.where(lane == 98, rate[:, 0:1], jnp.where(lane == 99, rate[:, 8:9], misc))
+        if ch >= 8:
+            misc = jnp.zeros((32, 128), F32)
         mixed_ref[at, :] = jnp.where(
             lane < 32,
             query[at],
@@ -204,13 +207,15 @@
         value[0:256],
         jnp.where(wide < 64, value[256:512], jnp.where(wide < 96, value[512:768], value[768:1024])),
     )
+    lane8 = lanes((8, 128))
     for slot in range(32):
         sums = mixed_ref[pl.ds(heads_ref[slot], 24, stride=32), :]
-        out_ref[slot, 0:16, :] = sums[0:16].astype(BF16)
-        rest = left_of_both(sums[0:16])
+        tile = jnp.where(lane8 < 96, sums[8:16], pltpu.roll(late_rest_ref[slot], 96, 1))
+        pair = jnp.concatenate([sums[0:8], tile], axis=0)
+        out_ref[slot, 0:16, :] = pair.astype(BF16)
+        rest = left_of_both(pair)
         out_ref[slot, 16:32, :] = jnp.concatenate([rest, sums[16:24]], axis=0).astype(BF16)
     out_ref[:, 32:48, :] = late_ref[...]
-    out_ref[:, 48:56, :] = late_rest_ref[...]
 
 
 def spread(array, base):
@@ -233,9 +238,10 @@
             total = part if total is None else total + part
         mixed.append(total)
     mixed = jnp.concatenate(mixed, axis=0)
-    below = pltpu.roll(mixed, 127, 0)
     channel = rows_of((128, 1)) % 16
-    rate = jnp.where(channel == 0, below[:, 97:98], mixed[:, 96:97])
+    rate = jnp.where(channel == 0, pltpu.roll(mixed, 127, 0)[:, 98:99], mixed[:, 96:97])
+    rate = jnp.where(channel == 8, pltpu.roll(mixed, 7, 0)[:, 99:100], rate)
+    rate = jnp.where(channel > 8, pltpu.roll(mixed, 8, 0)[:, 97:98], rate)
     soft = jnp.maximum(mixed, 0.0) + jnp.log1p(jnp.exp(-jnp.abs(mixed)))
     alpha = jnp.exp(-rate * soft)
     key_size = jnp.sum(mixed * mixed, axis=0, keepdims=True)
@@ -257,10 +263,11 @@
         for r in range(8):
             at = slice(r * 16, r * 16 + 16)
             peer = 4 * r + c
-            rest = packed_ref[peer, 16:32, :].astype(F32)[0:8]
-            first, second = joined(packed_ref[peer, 0:16, :].astype(F32), rest)
+            rest = packed_ref[peer, 16:32, :].astype(F32)
+            first, second = joined(packed_ref[peer, 0:16, :].astype(F32), rest[0:8])
             state_ref[c, at, :] = jnp.concatenate([first, second], axis=0)
-            rest = arrived_ref[peer, 48:56, :].astype(F32)
+            tile = arrived_ref[peer, 0:16, :].astype(F32)[8:16]
+            rest = jnp.where(lane8 < 32, pltpu.roll(tile, 32, 1), rest[8:16])
             first, second = joined(arrived_ref[peer, 32:48, :].astype(F32), rest)
             state_ref[4 + c, at, :] = jnp.concatenate([first, second], axis=0)
             part = arrived_ref[peer, 16:32, :].astype(F32)[8:16]
@@ -428,7 +435,7 @@
             on_chip((32, 16, 128), BF16),
             on_chip((32, 8, 128), F32),
             on_chip((32, 16, 128), BF16),
-            on_chip((32, 8, 128), BF16),
+            on_chip((32, 8, 128), F32),
         ),
         in_specs=[VMEM],
         out_specs=(VMEM, VMEM, VMEM, VMEM),
@@ -440,16 +447,16 @@
     packed = pl.pallas_call(
         add_tokens_kernel,
         out_shape=on_chip((32, 48, 128), BF16),
-        in_specs=[VMEM, VMEM, VMEM],
+        in_specs=[VMEM, VMEM, VMEM, VMEM],
         out_specs=VMEM,
         interpret=INTERPRET,
         compiler_params=pltpu.CompilerParams(vmem_limit_bytes=16 << 20),
         name="add_tokens",
-    )(arrived, kept(early), kept(early_rest))
+    )(arrived, kept(early), kept(early_rest), kept(late_rest))
     packed = exchange(packed, BOTH)
     projected = pl.pallas_call(
         project_kernel,
-        out_shape=on_chip((32, 56, 128), BF16),
+        out_shape=on_chip((32, 48, 128), BF16),
         in_specs=[SMEM] + [VMEM] * 11,
         out_specs=VMEM,
         scratch_shapes=[pltpu.VMEM((768, 128), F32)],

time: 92.6 us -> 90.9 us (0.982)
  blocking collectives: 61.9 us -> 60.1 us
    all_to_all x3, blocking collectives: 61.9 us -> 60.1 us  [exchange(): array = lax.all_to_all(array, axis, split_axis=0, concat_axis=0, tiled=True)]
where the time goes in v6:
time: 90.9 us; the launch traced here: 90.6 us
  blocking collectives  60.1 us (66%)
  Pallas kernels  11.3 us (12%)
  starting transfers between devices  10.6 us (12%)
  waiting for transfers between devices  6.21 us (7%)
  local copies, waits for them, and re-layouts  1.64 us (2%)
    all_to_all x3, blocking collectives, exchange(): array = lax.all_to_all(array, axis, split_axis=0, concat_axis=0, tiled=True)  60.1 us
    all_to_all x1, starting transfers between devices, exchange(): array = lax.all_to_all(array, axis, split_axis=0, concat_axis=0, tiled=True)  10.6 us
    all_to_all x1, waiting for transfers between devices, exchange(): array = lax.all_to_all(array, axis, split_axis=0, concat_axis=0, tiled=True)  6.21 us
    pallas_call x1, Pallas kernels, shards(): pl.pallas_call(pick_kernel, out_shape=on_chip((groups, 32, 128), BF16), i...  3.41 us
    pallas_call x1, Pallas kernels, shards(): pl.pallas_call(finish_kernel, out_shape=(shape_of((8, 4, 32, 32), BF16),...  3 us
    pallas_call x1, Pallas kernels, shards(): pl.pallas_call(project_kernel, out_shape=on_chip((32, 48, 128), BF16), in...  2 us
    pallas_call x1, Pallas kernels, shards(): pl.pallas_call(steps_kernel, out_shape=on_chip((32, 32, 128), BF16), in_s...  1.94 us
  transfers between devices with their start and end apart: 1, of which 1 were waited for; matrix products, arithmetic and copies ran while one was open for 0% of the time, Pallas kernels for 1%

profile of v6, /device:TPU:8, one launch (start us, length us, event | category | flops | bytes accessed | tf_op | source)
XLA Modules:
  0.0 90.6 jit_solution(10430023689511394301)
XLA Ops:
  0.6 3.4 %pick.1 = bf16[16,32,128]{2,1,0:T(8,128)(2,1)} custom-call(s32[4,128]{1,0:T(4,128)} %bitcast.21, bf16[72,5120]{1,0:T(8,128)(2,1)} %bitcast.20), custom_call_target="tpu_custom_call" | custom-call | tf_op jit(solution)/shard_map/pick/pallas_call | solution.py:416
  4.0 0.0 copy-start.5
  4.1 0.0 copy-start.7
  4.1 0.0 copy-start.8
  4.1 0.0 copy-start.9
  4.1 0.0 copy-start.10
  4.1 10.6 %all-to-all-start = ((bf16[16,32,128]{2,1,0:T(8,128)(2,1)}), bf16[16,32,128]{2,1,0:T(8,128)(2,1)S(1)}, u32[]{:S(2)}, u32[]{:S(2)}) async-start(bf16[16,32,128]{2,1,0:T(8,128)(2,1)} %pick.1), calls=%async_computation | async-start | bytes 262144 | tf_op jit(solution)/shard_map/all_to_all | solution.py:32
  14.7 0.0 copy-start
  14.7 1.6 %copy-done = f32[8,16,32,32]{3,2,1,0:T(8,128)S(1)} copy-done((f32[8,16,32,32]{3,2,1,0:T(8,128)S(1)}, f32[8,16,32,32]{3,2,1,0:T(8,128)}, u32[]{:S(2)}) %copy-start) | copy-done | bytes 524312
  16.3 0.0 copy-start.2
  16.3 0.0 copy-start.3
  16.3 0.0 copy-start.4
  16.3 0.8 pack_state.1
  17.1 6.2 %all-to-all-done.arrived_ref = bf16[16,32,128]{2,1,0:T(8,128)(2,1)S(1)} async-done(((bf16[16,32,128]{2,1,0:T(8,128)(2,1)}), bf16[16,32,128]{2,1,0:T(8,128)(2,1)S(1)}, u32[]{:S(2)}, u32[]{:S(2)}) %all-to-all-start) | async-done | bytes 131104 | tf_op jit(solution)/shard_map/all_to_all | solution.py:32
  23.3 0.1 add_tokens.1
  23.4 25.4 %all_to_all.20.arrived_ref.packed_ref = bf16[32,48,128]{2,1,0:T(8,128)(2,1)S(1)} all-to-all(bf16[32,48,128]{2,1,0:T(8,128)(2,1)S(1)} %add_tokens.1), channel_id=1, replica_groups=mesh['dp'=16,'row'=8,'col'=4] {'row','col'}, dimensions={0} | all-to-all | bytes 786432 | tf_op jit(solution)/shard_map/all_to_all | solution.py:32
  48.8 0.0 copy-done.5
  48.8 0.0 copy-done.7
  48.8 0.0 copy-done.8
  48.8 0.0 copy-done.9
  48.8 0.0 copy-done.10
  48.8 0.0 copy-done.2
  48.8 0.0 copy-done.3
  48.9 0.0 copy-done.4
  48.9 0.0 copy-done.6
  48.9 0.0 copy-start.1
  48.9 2.0 %project.1 = bf16[32,48,128]{2,1,0:T(8,128)(2,1)S(1)} custom-call(s32[32]{0:T(128)S(1)} %copy-done.10, bf16[32,48,128]{2,1,0:T(8,128)(2,1)S(1)} %all_to_all.20.arrived_ref.packed_ref, bf16[512,576]{1,0:T(8,128)(2,1)S(1)} %bitcast.16, bf16[512,576]{1,0:T(8,128)(2,1)S(1)} %bitcast.17, bf16[1024,288]{1,0:T(8,128)(2,1)S(1)} %bitcast.15, ...), custom_call_target="tpu_custom_call" | custom-call | tf_op jit(solution)/shard_map/project/pallas_call | solution.py:457
  50.9 19.0 %all_to_all.21.arrived_ref = bf16[32,48,128]{2,1,0:T(8,128)(2,1)S(1)} all-to-all(bf16[32,48,128]{2,1,0:T(8,128)(2,1)S(1)} %project.1), channel_id=1, replica_groups=mesh['dp'=16,'row'=8,'col'=4] {'row','col'}, dimensions={0} | all-to-all | bytes 786432 | tf_op jit(solution)/shard_map/all_to_all | solution.py:32
  69.8 1.9 %steps.1 = bf16[32,32,128]{2,1,0:T(8,128)(2,1)S(1)} custom-call(bf16[32,48,128]{2,1,0:T(8,128)(2,1)S(1)} %all_to_all.21.arrived_ref, bf16[32,48,128]{2,1,0:T(8,128)(2,1)S(1)} %all_to_all.20.arrived_ref.packed_ref), custom_call_target="tpu_custom_call" | custom-call | tf_op jit(solution)/shard_map/steps/pallas_call | solution.py:481
  71.8 15.8 %all_to_all.22.packed_ref = bf16[32,32,128]{2,1,0:T(8,128)(2,1)S(1)} all-to-all(bf16[32,32,128]{2,1,0:T(8,128)(2,1)S(1)} %steps.1), channel_id=1, replica_groups=mesh['dp'=16,'row'=8,'col'=4] {'row','col'}, dimensions={0} | all-to-all | bytes 524288 | tf_op jit(solution)/shard_map/all_to_all | solution.py:32
  87.6 0.0 copy-done.1
  87.6 3.0 %finish.1 = (bf16[8,4,32,32]{3,2,1,0:T(8,128)(2,1)}, f32[8,16,32,32]{3,2,1,0:T(8,128)}) custom-call(s32[32]{0:T(128)S(1)} %copy-done.10, bf16[32,32,128]{2,1,0:T(8,128)(2,1)S(1)} %all_to_all.22.packed_ref, f32[8,16,32,32]{3,2,1,0:T(8,128)S(1)} %copy-done.1), custom_call_target="tpu_custom_call" | custom-call | tf_op jit(solution)/shard_map/finish/pallas_call | solution.py:498
  (1 shorter events, 0.0 us)
Async XLA Ops:
  4.0 44.8 %copy-start.5 = (bf16[576,128]{1,0:T(8,128)(2,1)S(1)}, bf16[576,128]{1,0:T(8,128)(2,1)}, u32[]{:S(2)}) copy-start(bf16[576,128]{1,0:T(8,128)(2,1)} %down_ref.1) | copy-start | bytes 442372
  4.1 44.7 %copy-start.7 = (bf16[576,32]{0,1:T(8,128)(2,1)S(1)}, bf16[576,32]{0,1:T(8,128)(2,1)}, u32[]{:S(2)}) copy-start(bf16[576,32]{0,1:T(8,128)(2,1)} %param.22) | copy-start | bytes 110596
  4.1 44.7 %copy-start.8 = (f32[16,32]{1,0:T(8,128)S(1)}, f32[16,32]{1,0:T(8,128)}, u32[]{:S(2)}) copy-start(f32[16,32]{1,0:T(8,128)} %bias_ref.1) | copy-start | bytes 6148
  4.1 44.7 %copy-start.9 = (f32[16,32]{1,0:T(8,128)S(1)}, f32[16,32]{1,0:T(8,128)}, u32[]{:S(2)}) copy-start(f32[16,32]{1,0:T(8,128)} %rate_ref.1) | copy-start | bytes 6148
  4.1 44.7 %copy-start.10 = (s32[32]{0:T(128)S(1)}, s32[32]{0:T(128)}, u32[]{:S(2)}) copy-start(s32[32]{0:T(128)} %heads_ref.3) | copy-start | bytes 388
  4.1 19.2 %all-to-all-start = ((bf16[16,32,128]{2,1,0:T(8,128)(2,1)}), bf16[16,32,128]{2,1,0:T(8,128)(2,1)S(1)}, u32[]{:S(2)}, u32[]{:S(2)}) async-start(bf16[16,32,128]{2,1,0:T(8,128)(2,1)} %pick.1), calls=%async_computation | async-start | bytes 262144 | tf_op jit(solution)/shard_map/all_to_all | solution.py:32
  14.7 1.6 %copy-start = (f32[8,16,32,32]{3,2,1,0:T(8,128)S(1)}, f32[8,16,32,32]{3,2,1,0:T(8,128)}, u32[]{:S(2)}) copy-start(f32[8,16,32,32]{3,2,1,0:T(8,128)} %state_ref.3) | copy-start | bytes 1572868
  16.3 32.6 %copy-start.2 = (bf16[288,32,32]{0,2,1:T(8,128)(2,1)S(1)}, bf16[288,32,32]{0,2,1:T(8,128)(2,1)}, u32[]{:S(2)}) copy-start(bf16[288,32,32]{0,2,1:T(8,128)(2,1)} %param.17) | copy-start | bytes 1769476
  16.3 32.6 %copy-start.3 = (bf16[576,16,32]{0,2,1:T(8,128)(2,1)S(1)}, bf16[576,16,32]{0,2,1:T(8,128)(2,1)}, u32[]{:S(2)}) copy-start(bf16[576,16,32]{0,2,1:T(8,128)(2,1)} %param.15) | copy-start | bytes 1769476
  16.3 32.6 %copy-start.4 = (bf16[576,16,32]{0,2,1:T(8,128)(2,1)S(1)}, bf16[576,16,32]{0,2,1:T(8,128)(2,1)}, u32[]{:S(2)}) copy-start(bf16[576,16,32]{0,2,1:T(8,128)(2,1)} %param.16) | copy-start | bytes 1769476
  16.3 32.6 %copy-start.6 = (bf16[128,16,32]{0,2,1:T(8,128)(2,1)S(1)}, bf16[128,16,32]{0,2,1:T(8,128)(2,1)}, u32[]{:S(2)}) copy-start(bf16[128,16,32]{0,2,1:T(8,128)(2,1)} %param.19) | copy-start | bytes 393220
  48.9 38.7 %copy-start.1 = (f32[8,16,32,32]{3,2,1,0:T(8,128)S(1)}, f32[8,16,32,32]{3,2,1,0:T(8,128)}, u32[]{:S(2)}) copy-start(f32[8,16,32,32]{3,2,1,0:T(8,128)} %state_ref.3) | copy-start | bytes 1572868

commit v7 on v6

--- a/solution.py
+++ b/solution.py
@@ -50,24 +50,30 @@
     ids_copy.start()
     table_copy.start()
     ids_copy.wait()
+    table_copy.wait()
     start = lax.axis_index("dp") * vocab
     wide = jnp.broadcast_to((ids_ref[...] - start).astype(F32)[:, None, :], (steps, 8, streams))
+    columns = [wide[t].T.astype(jnp.int32)[:, 0:1] for t in range(steps)]
     width = 1024
+    total = None
+    for part in range(vocab // width):
+        across = slice(part * width, (part + 1) * width)
+        for t in range(steps):
+            hit = columns[t] == lanes((streams, width)) + part * width
+            onehot_ref[t * streams : (t + 1) * streams, across] = jnp.where(hit, 1.0, 0.0).astype(BF16)
+        found = lax.dot_general(onehot_ref[:, across], table_ref[:, across], NT, preferred_element_type=F32)
+        total = found if total is None else total + found
+    total = jnp.concatenate([total, jnp.zeros((total.shape[0], 128 - feats), F32)], axis=1)
+    steps_rows = [total[t * streams : (t + 1) * streams] for t in range(steps)]
+    lane = lanes((streams, 128))
+    tail = jnp.zeros((streams, 128), F32)
     for t in range(steps):
-        column = wide[t].T.astype(jnp.int32)[:, 0:1]
-        for part in range(vocab // width):
-            hit = column == lanes((streams, width)) + part * width
-            onehot_ref[t * streams : (t + 1) * streams, part * width : (part + 1) * width] = jnp.where(
-                hit, 1.0, 0.0
-            ).astype(BF16)
-    table_copy.wait()
-    total = lax.dot_general(onehot_ref[...], table_ref[...], NT, preferred_element_type=F32)
-    total = jnp.concatenate([total, jnp.zeros((total.shape[0], 128 - feats), F32)], axis=1)
-    for t in range(0, steps, 2):
-        pair = [
-            total[k * streams : (k + 1) * streams].reshape(groups, 8, 128) for k in (t, t + 1)
-        ]
-        out_ref[:, t * 8 : t * 8 + 16, :] = jnp.concatenate(pair, axis=1).astype(BF16)
+        moved = pltpu.roll(steps_rows[t], 64 + 8 * t, 1)
+        tail = jnp.where((lane >= 8 * t) & (lane < 8 * t + 8), moved, tail)
+    main = [jnp.where(lane < 64, steps_rows[t], pltpu.roll(steps_rows[t + 2], 64, 1)) for t in range(2)]
+    main = [part.reshape(groups, 8, 128) for part in main]
+    out_ref[:, 0:16, :] = jnp.concatenate(main, axis=1).astype(BF16)
+    out_ref[:, 16:24, :] = tail.reshape(groups, 8, 128).astype(BF16)
 
 
 LEVELS = 10
@@ -113,13 +119,9 @@
     own = arrived_ref[0].astype(F32)
     for k in range(1, arrived_ref.shape[0]):
         own = own + arrived_ref[k].astype(F32)
-    lane16 = lanes((16, 128))
     lane8 = lanes((8, 128))
-    main = jnp.where(lane16 < 64, own[0:16], pltpu.roll(own[16:32], 64, 1)).astype(BF16)
-    tail = jnp.zeros((8, 128), F32)
-    for k in range(4):
-        moved = pltpu.roll(own[8 * k : 8 * k + 8], 64 + 8 * k, 1)
-        tail = jnp.where((lane8 >= 8 * k) & (lane8 < 8 * k + 8), moved, tail)
+    main = own[0:16].astype(BF16)
+    tail = own[16:24]
     out_ref[:, 0:16, :] = early_ref[...]
     for p in range(out_ref.shape[0]):
         spare = jnp.where(lane8 < 32, tail, late_rest_ref[p])
@@ -415,7 +417,7 @@
     table = embed_table.T
     picked = pl.pallas_call(
         pick_kernel,
-        out_shape=on_chip((groups, 32, 128), BF16),
+        out_shape=on_chip((groups, 24, 128), BF16),
         in_specs=[ANY, ANY],
         out_specs=VMEM,
         scratch_shapes=[

time: 90.9 us -> 90.5 us (level)
  no operation moved by 1% of the time
where the time goes in v7:
time: 90.5 us; the launch traced here: 90.2 us
  blocking collectives  59.9 us (66%)
  Pallas kernels  11.4 us (13%)
  starting transfers between devices  10.6 us (12%)
  waiting for transfers between devices  5.84 us (6%)
  local copies, waits for them, and re-layouts  1.64 us (2%)
    all_to_all x3, blocking collectives, exchange(): array = lax.all_to_all(array, axis, split_axis=0, concat_axis=0, tiled=True)  59.9 us
    all_to_all x1, starting transfers between devices, exchange(): array = lax.all_to_all(array, axis, split_axis=0, concat_axis=0, tiled=True)  10.6 us
    all_to_all x1, waiting for transfers between devices, exchange(): array = lax.all_to_all(array, axis, split_axis=0, concat_axis=0, tiled=True)  5.84 us
    pallas_call x1, Pallas kernels, shards(): pl.pallas_call(pick_kernel, out_shape=on_chip((groups, 24, 128), BF16), i...  3.63 us
    pallas_call x1, Pallas kernels, shards(): pl.pallas_call(finish_kernel, out_shape=(shape_of((8, 4, 32, 32), BF16),...  3 us
    pallas_call x1, Pallas kernels, shards(): pl.pallas_call(project_kernel, out_shape=on_chip((32, 48, 128), BF16), in...  1.99 us
    pallas_call x1, Pallas kernels, shards(): pl.pallas_call(steps_kernel, out_shape=on_chip((32, 32, 128), BF16), in_s...  1.94 us
  transfers between devices with their start and end apart: 1, of which 1 were waited for; matrix products, arithmetic and copies ran while one was open for 0% of the time, Pallas kernels for 1%

profile of v7, /device:TPU:8, one launch (start us, length us, event | category | flops | bytes accessed | tf_op | source)
XLA Modules:
  0.0 90.2 jit_solution(11090826492854094150)
XLA Ops:
  0.6 3.6 %pick.1 = bf16[16,24,128]{2,1,0:T(8,128)(2,1)} custom-call(s32[4,128]{1,0:T(4,128)} %bitcast.21, bf16[72,5120]{1,0:T(8,128)(2,1)} %bitcast.20), custom_call_target="tpu_custom_call" | custom-call | tf_op jit(solution)/shard_map/pick/pallas_call | solution.py:418
  4.3 0.0 copy-start.5
  4.3 0.0 copy-start.7
  4.3 0.0 copy-start.8
  4.3 10.6 %all-to-all-start = ((bf16[16,24,128]{2,1,0:T(8,128)(2,1)}), bf16[16,24,128]{2,1,0:T(8,128)(2,1)S(1)}, u32[]{:S(2)}, u32[]{:S(2)}) async-start(bf16[16,24,128]{2,1,0:T(8,128)(2,1)} %pick.1), calls=%async_computation | async-start | bytes 196608 | tf_op jit(solution)/shard_map/all_to_all | solution.py:32
  14.9 0.0 copy-start
  14.9 1.6 %copy-done = f32[8,16,32,32]{3,2,1,0:T(8,128)S(1)} copy-done((f32[8,16,32,32]{3,2,1,0:T(8,128)S(1)}, f32[8,16,32,32]{3,2,1,0:T(8,128)}, u32[]{:S(2)}) %copy-start) | copy-done | bytes 524312
  16.5 0.0 copy-start.2
  16.5 0.0 copy-start.3
  16.5 0.0 copy-start.4
  16.5 0.0 copy-start.6
  16.5 0.0 copy-start.9
  16.5 0.0 copy-start.10
  16.5 0.8 pack_state.1
  17.3 5.8 %all-to-all-done.arrived_ref = bf16[16,24,128]{2,1,0:T(8,128)(2,1)S(1)} async-done(((bf16[16,24,128]{2,1,0:T(8,128)(2,1)}), bf16[16,24,128]{2,1,0:T(8,128)(2,1)S(1)}, u32[]{:S(2)}, u32[]{:S(2)}) %all-to-all-start) | async-done | bytes 98336 | tf_op jit(solution)/shard_map/all_to_all | solution.py:32
  23.2 25.3 %all_to_all.20.arrived_ref.packed_ref = bf16[32,48,128]{2,1,0:T(8,128)(2,1)S(1)} all-to-all(bf16[32,48,128]{2,1,0:T(8,128)(2,1)S(1)} %add_tokens.1), channel_id=1, replica_groups=mesh['dp'=16,'row'=8,'col'=4] {'row','col'}, dimensions={0} | all-to-all | bytes 786432 | tf_op jit(solution)/shard_map/all_to_all | solution.py:32
  48.5 0.0 copy-done.5
  48.5 0.0 copy-done.7
  48.5 0.0 copy-done.8
  48.5 0.0 copy-done.2
  48.5 0.0 copy-done.3
  48.6 0.0 copy-done.4
  48.6 0.0 copy-done.6
  48.6 0.0 copy-done.9
  48.6 0.0 copy-done.10
  48.6 0.0 copy-start.1
  48.6 2.0 %project.1 = bf16[32,48,128]{2,1,0:T(8,128)(2,1)S(1)} custom-call(s32[32]{0:T(128)S(1)} %copy-done.10, bf16[32,48,128]{2,1,0:T(8,128)(2,1)S(1)} %all_to_all.20.arrived_ref.packed_ref, bf16[512,576]{1,0:T(8,128)(2,1)S(1)} %bitcast.16, bf16[512,576]{1,0:T(8,128)(2,1)S(1)} %bitcast.17, bf16[1024,288]{1,0:T(8,128)(2,1)S(1)} %bitcast.15, ...), custom_call_target="tpu_custom_call" | custom-call | tf_op jit(solution)/shard_map/project/pallas_call | solution.py:459
  50.6 18.8 %all_to_all.21.arrived_ref = bf16[32,48,128]{2,1,0:T(8,128)(2,1)S(1)} all-to-all(bf16[32,48,128]{2,1,0:T(8,128)(2,1)S(1)} %project.1), channel_id=1, replica_groups=mesh['dp'=16,'row'=8,'col'=4] {'row','col'}, dimensions={0} | all-to-all | bytes 786432 | tf_op jit(solution)/shard_map/all_to_all | solution.py:32
  69.4 1.9 %steps.1 = bf16[32,32,128]{2,1,0:T(8,128)(2,1)S(1)} custom-call(bf16[32,48,128]{2,1,0:T(8,128)(2,1)S(1)} %all_to_all.21.arrived_ref, bf16[32,48,128]{2,1,0:T(8,128)(2,1)S(1)} %all_to_all.20.arrived_ref.packed_ref), custom_call_target="tpu_custom_call" | custom-call | tf_op jit(solution)/shard_map/steps/pallas_call | solution.py:483
  71.4 15.8 %all_to_all.22.packed_ref = bf16[32,32,128]{2,1,0:T(8,128)(2,1)S(1)} all-to-all(bf16[32,32,128]{2,1,0:T(8,128)(2,1)S(1)} %steps.1), channel_id=1, replica_groups=mesh['dp'=16,'row'=8,'col'=4] {'row','col'}, dimensions={0} | all-to-all | bytes 524288 | tf_op jit(solution)/shard_map/all_to_all | solution.py:32
  87.2 0.0 copy-done.1
  87.2 3.0 %finish.1 = (bf16[8,4,32,32]{3,2,1,0:T(8,128)(2,1)}, f32[8,16,32,32]{3,2,1,0:T(8,128)}) custom-call(s32[32]{0:T(128)S(1)} %copy-done.10, bf16[32,32,128]{2,1,0:T(8,128)(2,1)S(1)} %all_to_all.22.packed_ref, f32[8,16,32,32]{3,2,1,0:T(8,128)S(1)} %copy-done.1), custom_call_target="tpu_custom_call" | custom-call | tf_op jit(solution)/shard_map/finish/pallas_call | solution.py:500
  (1 shorter events, 0.0 us)
Async XLA Ops:
  4.3 44.3 %copy-start.5 = (bf16[576,128]{1,0:T(8,128)(2,1)S(1)}, bf16[576,128]{1,0:T(8,128)(2,1)}, u32[]{:S(2)}) copy-start(bf16[576,128]{1,0:T(8,128)(2,1)} %down_ref.1) | copy-start | bytes 442372
  4.3 44.2 %copy-start.7 = (bf16[576,32]{0,1:T(8,128)(2,1)S(1)}, bf16[576,32]{0,1:T(8,128)(2,1)}, u32[]{:S(2)}) copy-start(bf16[576,32]{0,1:T(8,128)(2,1)} %param.22) | copy-start | bytes 110596
  4.3 44.2 %copy-start.8 = (f32[16,32]{1,0:T(8,128)S(1)}, f32[16,32]{1,0:T(8,128)}, u32[]{:S(2)}) copy-start(f32[16,32]{1,0:T(8,128)} %bias_ref.1) | copy-start | bytes 6148
  4.3 18.9 %all-to-all-start = ((bf16[16,24,128]{2,1,0:T(8,128)(2,1)}), bf16[16,24,128]{2,1,0:T(8,128)(2,1)S(1)}, u32[]{:S(2)}, u32[]{:S(2)}) async-start(bf16[16,24,128]{2,1,0:T(8,128)(2,1)} %pick.1), calls=%async_computation | async-start | bytes 196608 | tf_op jit(solution)/shard_map/all_to_all | solution.py:32
  14.9 1.6 %copy-start = (f32[8,16,32,32]{3,2,1,0:T(8,128)S(1)}, f32[8,16,32,32]{3,2,1,0:T(8,128)}, u32[]{:S(2)}) copy-start(f32[8,16,32,32]{3,2,1,0:T(8,128)} %state_ref.3) | copy-start | bytes 1572868
  16.5 32.1 %copy-start.2 = (bf16[288,32,32]{0,2,1:T(8,128)(2,1)S(1)}, bf16[288,32,32]{0,2,1:T(8,128)(2,1)}, u32[]{:S(2)}) copy-start(bf16[288,32,32]{0,2,1:T(8,128)(2,1)} %param.17) | copy-start | bytes 1769476
  16.5 32.1 %copy-start.3 = (bf16[576,16,32]{0,2,1:T(8,128)(2,1)S(1)}, bf16[576,16,32]{0,2,1:T(8,128)(2,1)}, u32[]{:S(2)}) copy-start(bf16[576,16,32]{0,2,1:T(8,128)(2,1)} %param.15) | copy-start | bytes 1769476
  16.5 32.1 %copy-start.4 = (bf16[576,16,32]{0,2,1:T(8,128)(2,1)S(1)}, bf16[576,16,32]{0,2,1:T(8,128)(2,1)}, u32[]{:S(2)}) copy-start(bf16[576,16,32]{0,2,1:T(8,128)(2,1)} %param.16) | copy-start | bytes 1769476
  16.5 32.1 %copy-start.6 = (bf16[128,16,32]{0,2,1:T(8,128)(2,1)S(1)}, bf16[128,16,32]{0,2,1:T(8,128)(2,1)}, u32[]{:S(2)}) copy-start(bf16[128,16,32]{0,2,1:T(8,128)(2,1)} %param.19) | copy-start | bytes 393220
  16.5 32.1 %copy-start.9 = (f32[16,32]{1,0:T(8,128)S(1)}, f32[16,32]{1,0:T(8,128)}, u32[]{:S(2)}) copy-start(f32[16,32]{1,0:T(8,128)} %rate_ref.1) | copy-start | bytes 6148
  16.5 32.1 %copy-start.10 = (s32[32]{0:T(128)S(1)}, s32[32]{0:T(128)}, u32[]{:S(2)}) copy-start(s32[32]{0:T(128)} %heads_ref.3) | copy-start | bytes 388
  48.6 38.6 %copy-start.1 = (f32[8,16,32,32]{3,2,1,0:T(8,128)S(1)}, f32[8,16,32,32]{3,2,1,0:T(8,128)}, u32[]{:S(2)}) copy-start(f32[8,16,32,32]{3,2,1,0:T(8,128)} %state_ref.3) | copy-start | bytes 1572868

commit v8 on v7

--- a/solution.py
+++ b/solution.py
@@ -50,19 +50,29 @@
     ids_copy.start()
     table_copy.start()
     ids_copy.wait()
-    table_copy.wait()
     start = lax.axis_index("dp") * vocab
     wide = jnp.broadcast_to((ids_ref[...] - start).astype(F32)[:, None, :], (steps, 8, streams))
     columns = [wide[t].T.astype(jnp.int32)[:, 0:1] for t in range(steps)]
     width = 1024
-    total = None
-    for part in range(vocab // width):
+    parts = vocab // width
+
+    def build(part):
         across = slice(part * width, (part + 1) * width)
         for t in range(steps):
             hit = columns[t] == lanes((streams, width)) + part * width
             onehot_ref[t * streams : (t + 1) * streams, across] = jnp.where(hit, 1.0, 0.0).astype(BF16)
+
+    ahead = 2
+    for part in range(ahead):
+        build(part)
+    table_copy.wait()
+    total = None
+    for part in range(parts):
+        across = slice(part * width, (part + 1) * width)
         found = lax.dot_general(onehot_ref[:, across], table_ref[:, across], NT, preferred_element_type=F32)
         total = found if total is None else total + found
+        if part + ahead < parts:
+            build(part + ahead)
     total = jnp.concatenate([total, jnp.zeros((total.shape[0], 128 - feats), F32)], axis=1)
     steps_rows = [total[t * streams : (t + 1) * streams] for t in range(steps)]
     lane = lanes((streams, 128))

time: 90.5 us -> 90.2 us (level)
  no operation moved by 1% of the time
where the time goes in v8:
time: 90.2 us; the launch traced here: 89.9 us
  blocking collectives  59.9 us (66%)
  Pallas kernels  11.2 us (12%)
  starting transfers between devices  10.6 us (12%)
  waiting for transfers between devices  5.84 us (6%)
  local copies, waits for them, and re-layouts  1.64 us (2%)
    all_to_all x3, blocking collectives, exchange(): array = lax.all_to_all(array, axis, split_axis=0, concat_axis=0, tiled=True)  59.9 us
    all_to_all x1, starting transfers between devices, exchange(): array = lax.all_to_all(array, axis, split_axis=0, concat_axis=0, tiled=True)  10.6 us
    all_to_all x1, waiting for transfers between devices, exchange(): array = lax.all_to_all(array, axis, split_axis=0, concat_axis=0, tiled=True)  5.84 us
    pallas_call x1, Pallas kernels, shards(): pl.pallas_call(pick_kernel, out_shape=on_chip((groups, 24, 128), BF16), i...  3.36 us
    pallas_call x1, Pallas kernels, shards(): pl.pallas_call(finish_kernel, out_shape=(shape_of((8, 4, 32, 32), BF16),...  3 us
    pallas_call x1, Pallas kernels, shards(): pl.pallas_call(project_kernel, out_shape=on_chip((32, 48, 128), BF16), in...  2 us
    pallas_call x1, Pallas kernels, shards(): pl.pallas_call(steps_kernel, out_shape=on_chip((32, 32, 128), BF16), in_s...  1.94 us
  transfers between devices with their start and end apart: 1, of which 1 were waited for; matrix products, arithmetic and copies ran while one was open for 0% of the time, Pallas kernels for 1%

profile of v8, /device:TPU:8, one launch (start us, length us, event | category | flops | bytes accessed | tf_op | source)
XLA Modules:
  0.0 89.9 jit_solution(1520555667492854477)
XLA Ops:
  0.6 3.4 %pick.1 = bf16[16,24,128]{2,1,0:T(8,128)(2,1)} custom-call(s32[4,128]{1,0:T(4,128)} %bitcast.21, bf16[72,5120]{1,0:T(8,128)(2,1)} %bitcast.20), custom_call_target="tpu_custom_call" | custom-call | tf_op jit(solution)/shard_map/pick/pallas_call | solution.py:428
  4.0 0.0 copy-start.5
  4.0 0.0 copy-start.7
  4.0 0.0 copy-start.8
  4.0 10.6 %all-to-all-start = ((bf16[16,24,128]{2,1,0:T(8,128)(2,1)}), bf16[16,24,128]{2,1,0:T(8,128)(2,1)S(1)}, u32[]{:S(2)}, u32[]{:S(2)}) async-start(bf16[16,24,128]{2,1,0:T(8,128)(2,1)} %pick.1), calls=%async_computation | async-start | bytes 196608 | tf_op jit(solution)/shard_map/all_to_all | solution.py:32
  14.6 0.0 copy-start
  14.6 1.6 %copy-done = f32[8,16,32,32]{3,2,1,0:T(8,128)S(1)} copy-done((f32[8,16,32,32]{3,2,1,0:T(8,128)S(1)}, f32[8,16,32,32]{3,2,1,0:T(8,128)}, u32[]{:S(2)}) %copy-start) | copy-done | bytes 524312
  16.2 0.0 copy-start.2
  16.2 0.0 copy-start.3
  16.2 0.0 copy-start.4
  16.2 0.0 copy-start.6
  16.2 0.0 copy-start.9
  16.2 0.0 copy-start.10
  16.2 0.8 pack_state.1
  17.1 5.8 %all-to-all-done.arrived_ref = bf16[16,24,128]{2,1,0:T(8,128)(2,1)S(1)} async-done(((bf16[16,24,128]{2,1,0:T(8,128)(2,1)}), bf16[16,24,128]{2,1,0:T(8,128)(2,1)S(1)}, u32[]{:S(2)}, u32[]{:S(2)}) %all-to-all-start) | async-done | bytes 98336 | tf_op jit(solution)/shard_map/all_to_all | solution.py:32
  23.0 25.3 %all_to_all.20.arrived_ref.packed_ref = bf16[32,48,128]{2,1,0:T(8,128)(2,1)S(1)} all-to-all(bf16[32,48,128]{2,1,0:T(8,128)(2,1)S(1)} %add_tokens.1), channel_id=1, replica_groups=mesh['dp'=16,'row'=8,'col'=4] {'row','col'}, dimensions={0} | all-to-all | bytes 786432 | tf_op jit(solution)/shard_map/all_to_all | solution.py:32
  48.3 0.0 copy-done.5
  48.3 0.0 copy-done.7
  48.3 0.0 copy-done.8
  48.3 0.0 copy-done.2
  48.3 0.0 copy-done.3
  48.3 0.0 copy-done.4
  48.3 0.0 copy-done.6
  48.3 0.0 copy-done.9
  48.3 0.0 copy-done.10
  48.3 0.0 copy-start.1
  48.3 2.0 %project.1 = bf16[32,48,128]{2,1,0:T(8,128)(2,1)S(1)} custom-call(s32[32]{0:T(128)S(1)} %copy-done.10, bf16[32,48,128]{2,1,0:T(8,128)(2,1)S(1)} %all_to_all.20.arrived_ref.packed_ref, bf16[512,576]{1,0:T(8,128)(2,1)S(1)} %bitcast.16, bf16[512,576]{1,0:T(8,128)(2,1)S(1)} %bitcast.17, bf16[1024,288]{1,0:T(8,128)(2,1)S(1)} %bitcast.15, ...), custom_call_target="tpu_custom_call" | custom-call | tf_op jit(solution)/shard_map/project/pallas_call | solution.py:469
  50.4 18.8 %all_to_all.21.arrived_ref = bf16[32,48,128]{2,1,0:T(8,128)(2,1)S(1)} all-to-all(bf16[32,48,128]{2,1,0:T(8,128)(2,1)S(1)} %project.1), channel_id=1, replica_groups=mesh['dp'=16,'row'=8,'col'=4] {'row','col'}, dimensions={0} | all-to-all | bytes 786432 | tf_op jit(solution)/shard_map/all_to_all | solution.py:32
  69.2 1.9 %steps.1 = bf16[32,32,128]{2,1,0:T(8,128)(2,1)S(1)} custom-call(bf16[32,48,128]{2,1,0:T(8,128)(2,1)S(1)} %all_to_all.21.arrived_ref, bf16[32,48,128]{2,1,0:T(8,128)(2,1)S(1)} %all_to_all.20.arrived_ref.packed_ref), custom_call_target="tpu_custom_call" | custom-call | tf_op jit(solution)/shard_map/steps/pallas_call | solution.py:493
  71.1 15.8 %all_to_all.22.packed_ref = bf16[32,32,128]{2,1,0:T(8,128)(2,1)S(1)} all-to-all(bf16[32,32,128]{2,1,0:T(8,128)(2,1)S(1)} %steps.1), channel_id=1, replica_groups=mesh['dp'=16,'row'=8,'col'=4] {'row','col'}, dimensions={0} | all-to-all | bytes 524288 | tf_op jit(solution)/shard_map/all_to_all | solution.py:32
  86.9 0.0 copy-done.1
  86.9 3.0 %finish.1 = (bf16[8,4,32,32]{3,2,1,0:T(8,128)(2,1)}, f32[8,16,32,32]{3,2,1,0:T(8,128)}) custom-call(s32[32]{0:T(128)S(1)} %copy-done.10, bf16[32,32,128]{2,1,0:T(8,128)(2,1)S(1)} %all_to_all.22.packed_ref, f32[8,16,32,32]{3,2,1,0:T(8,128)S(1)} %copy-done.1), custom_call_target="tpu_custom_call" | custom-call | tf_op jit(solution)/shard_map/finish/pallas_call | solution.py:510
  (1 shorter events, 0.0 us)
Async XLA Ops:
  4.0 44.3 %copy-start.5 = (bf16[576,128]{1,0:T(8,128)(2,1)S(1)}, bf16[576,128]{1,0:T(8,128)(2,1)}, u32[]{:S(2)}) copy-start(bf16[576,128]{1,0:T(8,128)(2,1)} %down_ref.1) | copy-start | bytes 442372
  4.0 44.3 %copy-start.7 = (bf16[576,32]{0,1:T(8,128)(2,1)S(1)}, bf16[576,32]{0,1:T(8,128)(2,1)}, u32[]{:S(2)}) copy-start(bf16[576,32]{0,1:T(8,128)(2,1)} %param.22) | copy-start | bytes 110596
  4.0 44.2 %copy-start.8 = (f32[16,32]{1,0:T(8,128)S(1)}, f32[16,32]{1,0:T(8,128)}, u32[]{:S(2)}) copy-start(f32[16,32]{1,0:T(8,128)} %bias_ref.1) | copy-start | bytes 6148
  4.0 18.9 %all-to-all-start = ((bf16[16,24,128]{2,1,0:T(8,128)(2,1)}), bf16[16,24,128]{2,1,0:T(8,128)(2,1)S(1)}, u32[]{:S(2)}, u32[]{:S(2)}) async-start(bf16[16,24,128]{2,1,0:T(8,128)(2,1)} %pick.1), calls=%async_computation | async-start | bytes 196608 | tf_op jit(solution)/shard_map/all_to_all | solution.py:32
  14.6 1.6 %copy-start = (f32[8,16,32,32]{3,2,1,0:T(8,128)S(1)}, f32[8,16,32,32]{3,2,1,0:T(8,128)}, u32[]{:S(2)}) copy-start(f32[8,16,32,32]{3,2,1,0:T(8,128)} %state_ref.3) | copy-start | bytes 1572868
  16.2 32.1 %copy-start.2 = (bf16[288,32,32]{0,2,1:T(8,128)(2,1)S(1)}, bf16[288,32,32]{0,2,1:T(8,128)(2,1)}, u32[]{:S(2)}) copy-start(bf16[288,32,32]{0,2,1:T(8,128)(2,1)} %param.17) | copy-start | bytes 1769476
  16.2 32.1 %copy-start.3 = (bf16[576,16,32]{0,2,1:T(8,128)(2,1)S(1)}, bf16[576,16,32]{0,2,1:T(8,128)(2,1)}, u32[]{:S(2)}) copy-start(bf16[576,16,32]{0,2,1:T(8,128)(2,1)} %param.15) | copy-start | bytes 1769476
  16.2 32.1 %copy-start.4 = (bf16[576,16,32]{0,2,1:T(8,128)(2,1)S(1)}, bf16[576,16,32]{0,2,1:T(8,128)(2,1)}, u32[]{:S(2)}) copy-start(bf16[576,16,32]{0,2,1:T(8,128)(2,1)} %param.16) | copy-start | bytes 1769476
  16.2 32.1 %copy-start.6 = (bf16[128,16,32]{0,2,1:T(8,128)(2,1)S(1)}, bf16[128,16,32]{0,2,1:T(8,128)(2,1)}, u32[]{:S(2)}) copy-start(bf16[128,16,32]{0,2,1:T(8,128)(2,1)} %param.19) | copy-start | bytes 393220
  16.2 32.1 %copy-start.9 = (f32[16,32]{1,0:T(8,128)S(1)}, f32[16,32]{1,0:T(8,128)}, u32[]{:S(2)}) copy-start(f32[16,32]{1,0:T(8,128)} %rate_ref.1) | copy-start | bytes 6148
  16.2 32.1 %copy-start.10 = (s32[32]{0:T(128)S(1)}, s32[32]{0:T(128)}, u32[]{:S(2)}) copy-start(s32[32]{0:T(128)} %heads_ref.3) | copy-start | bytes 388
  48.3 38.6 %copy-start.1 = (f32[8,16,32,32]{3,2,1,0:T(8,128)S(1)}, f32[8,16,32,32]{3,2,1,0:T(8,128)}, u32[]{:S(2)}) copy-start(f32[8,16,32,32]{3,2,1,0:T(8,128)} %state_ref.3) | copy-start | bytes 1572868
